TPU v7x, 128 devices: a whole 4x4x4 slice. The times are simulated.
128 devices in a mesh: block: 4 (over x), tok: 32 (over z, y, core).
Axes of the slice: x: 4, y: 4, z: 4, core: 2. Of those that a mesh axis runs over, the one named last changes fastest.
Arguments:
- keys: bfloat16 [4, 2, 8192, 1280], P('block', None, 'tok'), may hold values from -6 to 6
- values: bfloat16 [4, 2, 8192, 1280], P('block', None, 'tok'), may hold values from -6 to 6
- queries: bfloat16 [4, 2, 8192, 1280], P('block', None, 'tok'), may hold values from -6 to 6
- rates: bfloat16 [4, 2, 8192, 20], P('block', None, 'tok'), may hold values from 0.00049972534 to 0.0049743652
- counts: int32 [4, 2, 32, 20], P('block', None, 'tok'), may hold values from 1 to 256
- stagger: int32 [20], replicated, may hold values from 0 to 255
- gate_in: bfloat16 [4, 20, 64, 512], P('block', None, None, 'tok'), may hold values from -0.75 to 0.75
- up_in: bfloat16 [4, 20, 64, 512], P('block', None, None, 'tok'), may hold values from -0.75 to 0.75
- down_in: bfloat16 [4, 20, 64, 512], P('block', None, None, 'tok'), may hold values from -0.25 to 0.25
- entry_gate: bfloat16 [20, 64, 512], replicated, may hold values from -0.75 to 0.75
- entry_up: bfloat16 [20, 64, 512], replicated, may hold values from -0.75 to 0.75
- entry_down: bfloat16 [20, 64, 512], replicated, may hold values from -0.25 to 0.25
Outputs:
- answers: bfloat16 [4, 2, 8192, 1280], P('block', None, 'tok')
- gate_out: bfloat16 [4, 20, 64, 512], P('block', None, None, 'tok')
- up_out: bfloat16 [4, 20, 64, 512], P('block', None, None, 'tok')
- down_out: bfloat16 [4, 20, 64, 512], P('block', None, None, 'tok')
All inputs are finite; a program needn't handle non-finite values.
Results may differ from a plain program's by a relative error of at most 0.022.
Values may be sent and summed in bfloat16 or wider, within the bound.
No kernel may reach another device: no remote copies, remote signals or barrier semaphores. Data moves between devices by JAX's collectives and lax.ppermute only.
A program may use at most 320 MiB of HBM per device.

v0:
```python
import jax
import jax.numpy as jnp
from jax import lax
from jax.sharding import PartitionSpec as P

EPS = 1e-06


def as_sent(x):
    return jax.tree.map(lambda a: a.astype(jnp.bfloat16) if a.dtype == jnp.float32 else a, x)


def passed_along(value, axis, steps):
    count = lax.axis_size(axis)
    initial, last = (max(0, -steps), min(count, count - steps))
    return lax.ppermute(value, axis, [(source, source + steps) for source in range(initial, last)])


def side_by_side(arrays, axis, dim, along):
    widths = [a.shape[along] for a in arrays]
    both = jnp.concatenate(arrays, axis=along)
    result = lax.all_gather(both, axis, axis=dim, tiled=True)
    return tuple(jnp.split(result, [sum(widths[:k]) for k in range(1, len(widths))], axis=along))


def row_scale(rates_tick, counts_tick, stagger):
    rows = rates_tick.shape[0]
    offset = jnp.arange(rows, dtype=jnp.int32)[:, None]
    inside = jnp.mod(offset - stagger[None, :], rows)
    return jnp.where(inside < counts_tick[None, :], rates_tick, jnp.zeros_like(rates_tick))


def gradients(keys, values, scale, weights):
    gate_w, up_w, down_w = weights
    rows = keys.shape[0]
    heads = gate_w.shape[0]
    size = gate_w.shape[1]
    kk = keys.reshape(rows, heads, size)
    vv = values.reshape(rows, heads, size)
    pre_gate = jnp.einsum("rhd,hdf->rhf", kk, gate_w, preferred_element_type=jnp.float32)
    pre_up = jnp.einsum("rhd,hdf->rhf", kk, up_w, preferred_element_type=jnp.float32)
    back = jnp.einsum("rhd,hdf->rhf", vv, down_w, preferred_element_type=jnp.float32)
    weight = scale.astype(jnp.float32)[:, :, None]
    sig = jax.nn.sigmoid(pre_gate)
    act = pre_gate * sig
    hidden = (weight * act * pre_up).astype(jnp.bfloat16)
    d_gate = (weight * back * pre_up * sig * (1.0 + pre_gate * (1.0 - sig))).astype(jnp.bfloat16)
    d_up = (weight * back * act).astype(jnp.bfloat16)
    step_gate = jnp.einsum("rhd,rhf->hdf", kk, d_gate, preferred_element_type=jnp.float32)
    step_up = jnp.einsum("rhd,rhf->hdf", kk, d_up, preferred_element_type=jnp.float32)
    step_down = jnp.einsum("rhd,rhf->hdf", vv, hidden, preferred_element_type=jnp.float32)
    return (step_gate, step_up, step_down)


def renew(weights, steps):
    result = []
    for weight, step in zip(weights, steps):
        base = weight.astype(jnp.float32)
        moved = base + step
        before = jnp.sqrt(jnp.sum(base * base, axis=1, keepdims=True) + EPS)
        after = jnp.sqrt(jnp.sum(moved * moved, axis=1, keepdims=True) + EPS)
        result.append((moved * (before / after)).astype(jnp.bfloat16))
    return tuple(result)


def respond(queries, weights):
    gate_w, up_w, down_w = weights
    rows = queries.shape[0]
    heads = gate_w.shape[0]
    size = gate_w.shape[1]
    qq = queries.reshape(rows, heads, size)
    pre_gate = jnp.einsum("rhd,hdf->rhf", qq, gate_w, preferred_element_type=jnp.float32)
    pre_up = jnp.einsum("rhd,hdf->rhf", qq, up_w, preferred_element_type=jnp.float32)
    hidden = (jax.nn.silu(pre_gate) * pre_up).astype(jnp.bfloat16)
    output = jnp.einsum("rhf,hdf->rhd", hidden, down_w, preferred_element_type=jnp.float32)
    return output.reshape(rows, heads * size)


def own_slice(whole, width):
    start = lax.axis_index("tok") * width
    return tuple((lax.dynamic_slice_in_dim(w, start, width, 2) for w in whole))


def pass_on(renewed, entry_shares):
    received = jax.tree.map(
        lambda part, own: part.astype(own.dtype),
        passed_along(as_sent(renewed), "block", 1),
        renewed,
    )
    first = lax.axis_index("block") == 0
    return tuple((jnp.where(first, e, g) for e, g in zip(entry_shares, received)))


def shards(
    keys,
    values,
    queries,
    rates,
    counts,
    stagger,
    gate_in,
    up_in,
    down_in,
    entry_gate,
    entry_up,
    entry_down,
):
    ticks = keys.shape[1]
    width = gate_in.shape[3]
    entry_whole = (entry_gate, entry_up, entry_down)
    entry_shares = own_slice(entry_whole, width)
    current = (gate_in[0], up_in[0], down_in[0])
    collected = []
    for tick in range(ticks):
        scale = row_scale(rates[0, tick], counts[0, tick, 0], stagger)
        all_keys, all_values, all_scale = side_by_side(
            (keys[0, tick], values[0, tick], scale), "tok", 0, 1
        )
        terms = gradients(all_keys, all_values, all_scale, current)
        renewed = renew(current, terms)
        full_new = jax.tree.map(
            lambda part, own: part.astype(own.dtype),
            lax.all_gather(as_sent(renewed), "tok", axis=2, tiled=True),
            renewed,
        )
        collected.append(respond(queries[0, tick], full_new).astype(jnp.bfloat16))
        current = renewed
        if tick + 1 < ticks:
            current = pass_on(renewed, entry_shares)
    answers = jnp.stack(collected, axis=0)[None]
    return (answers, current[0][None], current[1][None], current[2][None])


def solution(mesh):
    placed = (
        P("block", None, "tok", None),
        P("block", None, "tok", None),
        P("block", None, "tok", None),
        P("block", None, "tok", None),
        P("block", None, "tok", None),
        P(),
        P("block", None, None, "tok"),
        P("block", None, None, "tok"),
        P("block", None, None, "tok"),
        P(),
        P(),
        P(),
    )
    return jax.shard_map(
        shards,
        mesh=mesh,
        in_specs=placed,
        out_specs=(
            P("block", None, "tok", None),
            P("block", None, None, "tok"),
            P("block", None, None, "tok"),
            P("block", None, None, "tok"),
        ),
        check_vma=False,
    )
```

profile of v0, /device:TPU:7, one launch (start us, length us, event | category | flops | bytes accessed | tf_op | source)
XLA Modules:
  0.0 624.6 jit_solution(2055640495452974893)
XLA Ops:
  29.7 141.2 %all-gather.9.cloned.1.call-done = bf16[8192,2580]{0,1:T(8,128)(2,1)} async-done(((bf16[256,2580]{0,1:T(8,128)(2,1)}), bf16[8192,2580]{0,1:T(8,128)(2,1)}) %all-gather.9.cloned.1.call-update) | async-done | bytes 42270736 | tf_op jit(solution)/shard_map/all_gather | solution.py:22
  171.9 28.4 %fusion.66 = (bf16[8192,1280]{0,1:T(8,128)(2,1)}, bf16[8192,1280]{0,1:T(8,128)(2,1)}) fusion(bf16[8192,2580]{0,1:T(8,128)(2,1)} %all-gather.9.cloned.1.call-done), kind=kLoop, calls=%fused_computation.118 | loop fusion | bytes 83886080 | tf_op jit(solution)/shard_map/split | solution.py:23
  200.3 13.4 %convolution_bitcast_fusion.2 = f32[8192,20,16]{0,2,1:T(8,128)} fusion(bf16[8192,20,64]{0,2,1:T(8,128)(2,1)} %bitcast.142, bf16[1,20,64,16]{2,3,1,0:T(8,128)(2,1)S(1)} %copy-done.7), kind=kOutput, calls=%fused_computation.2 | convolution fusion | flops 335544320 | bytes 31498240 | tf_op jit(solution)/shard_map/rhd,hdf->rhf/dot_general | solution.py:40
  222.6 15.0 %fusion.11 = f32[8192,20,16]{0,2,1:T(8,128)} fusion(bf16[8192,20,64]{0,2,1:T(8,128)(2,1)} %bitcast.146, f32[8192,20]{0,1:T(8,128)S(1)} %slice_convert_fusion.1, bf16[1,20,64,16]{2,3,1,0:T(8,128)(2,1)S(1)} %copy-done.6), kind=kOutput, calls=%fused_computation.31 | convolution fusion | flops 338165760 | bytes 32153600 | tf_op jit(solution)/shard_map/rhd,hdf->rhf/dot_general | solution.py:42
  237.7 18.3 %multiply_reduce_fusion.4 = (f32[20,16]{1,0:T(8,128)S(1)}, f32[20,64,16]{1,2,0:T(8,128)S(1)}) fusion(bf16[8192,20,64]{0,2,1:T(8,128)(2,1)} %bitcast.143, f32[8192,20,16]{0,2,1:T(8,128)} %convolution_bitcast_fusion.2, f32[8192,20,16]{0,2,1:T(8,128)} %fusion.11, f32[8192,20,16]{0,2,1:T(8,128)} %convolution_bitcast_fusion.1, ...), kind=kOutput, calls=%fused_computation.78 | convolution fusion | flops 361840320 | bytes 52552960 | tf_op jit(solution)/shard_map/rhd,rhf->hdf/dot_general | solution.py:49
  257.8 16.6 %multiply_reduce_fusion.3 = (f32[20,16]{1,0:T(8,128)S(1)}, f32[20,64,16]{1,2,0:T(8,128)S(1)}) fusion(bf16[8192,20,64]{0,2,1:T(8,128)(2,1)} %bitcast.144, f32[8192,20,16]{0,2,1:T(8,128)} %fusion.11, f32[8192,20,16]{0,2,1:T(8,128)} %convolution_bitcast_fusion.2, bf16[1,20,64,16]{2,3,1,0:T(8,128)(2,1)S(1)} %copy-done.8), kind=kOutput, calls=%fused_computation.76 | convolution fusion | flops 351354560 | bytes 42067200 | tf_op jit(solution)/shard_map/rhd,rhf->hdf/dot_general | solution.py:50
  275.9 17.7 %multiply_reduce_fusion.5 = (f32[20,16]{1,0:T(8,128)S(1)}, f32[20,64,16]{1,2,0:T(8,128)S(1)}) fusion(bf16[8192,20,64]{0,2,1:T(8,128)(2,1)} %bitcast.147, f32[8192,20,16]{0,2,1:T(8,128)} %convolution_bitcast_fusion.1, f32[8192,20]{0,1:T(8,128)S(1)} %slice_convert_fusion.1, f32[8192,20,16]{0,2,1:T(8,128)} %convolution_bitcast_fusion.2, ...), kind=kOutput, calls=%fused_computation.80 | convolution fusion | flops 353976000 | bytes 42722560 | tf_op jit(solution)/shard_map/rhd,rhf->hdf/dot_general | solution.py:51
  295.2 27.7 %all-gather.17.cloned.1.call-done = bf16[8192,2580]{0,1:T(8,128)(2,1)} async-done(((bf16[256,2580]{0,1:T(8,128)(2,1)}), bf16[8192,2580]{0,1:T(8,128)(2,1)}) %all-gather.17.cloned.1.call-update) | async-done | bytes 42270736 | tf_op jit(solution)/shard_map/all_gather | solution.py:22
  322.9 28.8 %fusion.65 = (bf16[8192,1280]{0,1:T(8,128)(2,1)}, bf16[8192,1280]{0,1:T(8,128)(2,1)}) fusion(bf16[8192,2580]{0,1:T(8,128)(2,1)} %all-gather.17.cloned.1.call-done), kind=kLoop, calls=%fused_computation.117 | loop fusion | bytes 83886080 | tf_op jit(solution)/shard_map/split | solution.py:23
  352.9 13.4 %convolution_bitcast_fusion.4 = f32[8192,20,16]{0,2,1:T(8,128)} fusion(bf16[20,64,16]{1,2,0:T(8,128)(2,1)S(1)} %get-tuple-element.5, bf16[8192,20,64]{0,2,1:T(8,128)(2,1)} %bitcast.138), kind=kOutput, calls=%fused_computation.4 | convolution fusion | flops 335544320 | bytes 31498240 | tf_op jit(solution)/shard_map/rhd,hdf->rhf/dot_general | solution.py:41
  370.0 5.5 convolution_bitcast_fusion.5
  375.6 11.9 %fusion.10 = f32[8192,20,16]{0,2,1:T(8,128)} fusion(bf16[20,64,16]{1,2,0:T(8,128)(2,1)S(1)} %get-tuple-element.9, bf16[8192,20,64]{0,2,1:T(8,128)(2,1)} %bitcast.148, f32[8192,20]{0,1:T(8,128)S(1)} %slice_convert_fusion), kind=kOutput, calls=%fused_computation.30 | convolution fusion | flops 338165760 | bytes 32153600 | tf_op jit(solution)/shard_map/rhd,hdf->rhf/dot_general | solution.py:42
  387.5 18.5 %multiply_reduce_fusion.1 = (f32[20,16]{1,0:T(8,128)S(1)}, f32[20,64,16]{1,2,0:T(8,128)S(1)}) fusion(bf16[8192,20,64]{0,2,1:T(8,128)(2,1)} %bitcast.139, f32[8192,20,16]{0,2,1:T(8,128)} %convolution_bitcast_fusion.5, f32[8192,20,16]{0,2,1:T(8,128)} %fusion.10, f32[8192,20,16]{0,2,1:T(8,128)} %convolution_bitcast_fusion.4, ...), kind=kOutput, calls=%fused_computation.72 | convolution fusion | flops 361840320 | bytes 52552960 | tf_op jit(solution)/shard_map/rhd,rhf->hdf/dot_general | solution.py:49
  406.8 10.9 %all-gather.19.cloned.1.call-start = ((), (), s32[]{:S(2)}) async-start(), calls=%async_computation.5 | async-start | bytes 2703360 | tf_op jit(solution)/shard_map/all_gather | solution.py:123
  417.7 15.4 %multiply_reduce_fusion.2 = (f32[20,16]{1,0:T(8,128)S(1)}, f32[20,64,16]{1,2,0:T(8,128)S(1)}) fusion(bf16[8192,20,64]{0,2,1:T(8,128)(2,1)} %bitcast.149, f32[8192,20,16]{0,2,1:T(8,128)} %convolution_bitcast_fusion.4, f32[8192,20]{0,1:T(8,128)S(1)} %slice_convert_fusion, f32[8192,20,16]{0,2,1:T(8,128)} %convolution_bitcast_fusion.5, ...), kind=kOutput, calls=%fused_computation.74 | convolution fusion | flops 353976000 | bytes 42722560 | tf_op jit(solution)/shard_map/rhd,rhf->hdf/dot_general | solution.py:51
  433.9 15.4 %multiply_reduce_fusion = (f32[20,16]{1,0:T(8,128)S(1)}, f32[20,64,16]{1,2,0:T(8,128)S(1)}) fusion(bf16[8192,20,64]{0,2,1:T(8,128)(2,1)} %bitcast.140, f32[8192,20,16]{0,2,1:T(8,128)} %fusion.10, f32[8192,20,16]{0,2,1:T(8,128)} %convolution_bitcast_fusion.5, bf16[20,64,16]{1,2,0:T(8,128)(2,1)S(1)} %get-tuple-element.5), kind=kOutput, calls=%fused_computation.70 | convolution fusion | flops 351354560 | bytes 42067200 | tf_op jit(solution)/shard_map/rhd,rhf->hdf/dot_general | solution.py:50
  452.4 7.3 %fusion.71 = f32[20,512,256]{2,1,0:T(8,128)} fusion(bf16[20,64,512]{1,2,0:T(8,128)(2,1)} %all-gather.13.cloned.1.call-done, bf16[256,20,64]{0,2,1:T(8,128)(2,1)S(1)} %bitcast.156), kind=kOutput, calls=%fused_computation.123 | convolution fusion | flops 335544320 | bytes 12451840 | tf_op jit(solution)/shard_map/rhd,hdf->rhf/dot_general | solution.py:72
  459.7 5.8 all-gather.11.cloned.1.call-done
  465.5 9.4 %fusion.35 = bf16[20,64,256]{2,1,0:T(8,128)(2,1)S(1)} fusion(bf16[20,64,512]{1,2,0:T(8,128)(2,1)} %all-gather.11.cloned.1.call-done, f32[20,512,256]{2,1,0:T(8,128)} %fusion.71, bf16[20,64,512]{1,2,0:T(8,128)(2,1)} %all-gather.15.cloned.1.call-done, bf16[256,20,64]{0,2,1:T(8,128)(2,1)S(1)} %bitcast.157), kind=kOutput, calls=%fused_computation.45 | convolution fusion | flops 687144960 | bytes 14417920 | tf_op jit(solution)/shard_map/rhf,hdf->rhd/dot_general | solution.py:75
  475.1 37.3 %all-gather.21.cloned.1.call-done = bf16[20,64,512]{1,2,0:T(8,128)(2,1)} async-done(((bf16[20,64,16]{1,2,0:T(8,128)(2,1)}), bf16[20,64,512]{1,2,0:T(8,128)(2,1)}) %all-gather.21.cloned.1.call-update) | async-done | bytes 1310736 | tf_op jit(solution)/shard_map/all_gather | solution.py:123
  512.5 7.2 %fusion.72 = f32[20,512,256]{2,1,0:T(8,128)} fusion(bf16[20,64,512]{1,2,0:T(8,128)(2,1)} %all-gather.21.cloned.1.call-done, bf16[256,20,64]{0,2,1:T(8,128)(2,1)S(1)} %bitcast.154), kind=kOutput, calls=%fused_computation.124 | convolution fusion | flops 335544320 | bytes 12451840 | tf_op jit(solution)/shard_map/rhd,hdf->rhf/dot_general | solution.py:72
  519.7 39.9 %all-gather.19.cloned.1.call-done = bf16[20,64,512]{1,2,0:T(8,128)(2,1)} async-done(((bf16[20,64,16]{1,2,0:T(8,128)(2,1)}), bf16[20,64,512]{1,2,0:T(8,128)(2,1)}) %all-gather.19.cloned.1.call-update) | async-done | bytes 1310736 | tf_op jit(solution)/shard_map/all_gather | solution.py:123
  559.6 47.1 %all-gather.23.cloned.1.call-done = bf16[20,64,512]{1,2,0:T(8,128)(2,1)} async-done(((bf16[20,64,16]{1,2,0:T(8,128)(2,1)}), bf16[20,64,512]{1,2,0:T(8,128)(2,1)}) %all-gather.23.cloned.1.call-update) | async-done | bytes 1310736 | tf_op jit(solution)/shard_map/all_gather | solution.py:123
  606.7 9.4 %fusion.32 = bf16[20,64,256]{2,1,0:T(8,128)(2,1)S(1)} fusion(bf16[20,64,512]{1,2,0:T(8,128)(2,1)} %all-gather.19.cloned.1.call-done, f32[20,512,256]{2,1,0:T(8,128)} %fusion.72, bf16[20,64,512]{1,2,0:T(8,128)(2,1)} %all-gather.23.cloned.1.call-done, bf16[256,20,64]{0,2,1:T(8,128)(2,1)S(1)} %bitcast.155), kind=kOutput, calls=%fused_computation.44 | convolution fusion | flops 687144960 | bytes 14417920 | tf_op jit(solution)/shard_map/rhf,hdf->rhd/dot_general | solution.py:75
  (100 shorter events, 48.3 us)
Async XLA Ops:
  7.2 13.8 %copy-start = (bf16[20,64,512]{2,1,0:T(8,128)(2,1)S(1)}, bf16[20,64,512]{2,1,0:T(8,128)(2,1)}, u32[]{:S(2)}) copy-start(bf16[20,64,512]{2,1,0:T(8,128)(2,1)} %param.21) | copy-start | bytes 3932164
  7.2 163.7 %all-gather.9.cloned.1.call-start = ((), (), s32[]{:S(2)}) async-start(), calls=%async_computation | async-start | bytes 43659264 | tf_op jit(solution)/shard_map/all_gather | solution.py:22
  13.8 15.5 %copy-start.7 = (bf16[1,20,64,16]{2,3,1,0:T(8,128)(2,1)S(1)}, bf16[1,20,64,16]{2,3,1,0:T(8,128)(2,1)}, u32[]{:S(2)}) copy-start(bf16[1,20,64,16]{2,3,1,0:T(8,128)(2,1)} %param.18) | copy-start | bytes 122884
  13.8 15.6 %copy-start.8 = (bf16[1,20,64,16]{2,3,1,0:T(8,128)(2,1)S(1)}, bf16[1,20,64,16]{2,3,1,0:T(8,128)(2,1)}, u32[]{:S(2)}) copy-start(bf16[1,20,64,16]{2,3,1,0:T(8,128)(2,1)} %param.19) | copy-start | bytes 122884
  13.8 15.8 %copy-start.6 = (bf16[1,20,64,16]{2,3,1,0:T(8,128)(2,1)S(1)}, bf16[1,20,64,16]{2,3,1,0:T(8,128)(2,1)}, u32[]{:S(2)}) copy-start(bf16[1,20,64,16]{2,3,1,0:T(8,128)(2,1)} %param.20) | copy-start | bytes 122884
  19.2 303.7 %all-gather.17.cloned.1.call-start = ((), (), s32[]{:S(2)}) async-start(), calls=%async_computation.4 | async-start | bytes 43659264 | tf_op jit(solution)/shard_map/all_gather | solution.py:22
  20.9 431.5 %all-gather.13.cloned.1.call-start = ((), (), s32[]{:S(2)}) async-start(), calls=%async_computation.2 | async-start | bytes 2703360 | tf_op jit(solution)/shard_map/all_gather | solution.py:123
  200.3 17.0 %copy-start.3 = (bf16[8192,1280]{0,1:T(8,128)(2,1)S(1)}, bf16[8192,1280]{0,1:T(8,128)(2,1)}, u32[]{:S(2)}) copy-start(bf16[8192,1280]{0,1:T(8,128)(2,1)} %get-tuple-element.13) | copy-start | bytes 62914564
  256.1 110.2 %collective-permute-start.1 = (bf16[20,64,16]{1,2,0:T(8,128)(2,1)S(1)}, bf16[20,64,16]{1,2,0:T(8,128)(2,1)S(1)}, u32[]{:S(2)}, u32[]{:S(2)}) collective-permute-start(bf16[20,64,16]{1,2,0:T(8,128)(2,1)S(1)} %multiply_convert_fusion.28), channel_id=1, source_target_pairs={{0,32},{32,64},{64,96},{1,33},{33,65},{65,97},{2,34},{34,66},{66,9... | collective-permute-start | bytes 122888 | tf_op jit(solution)/shard_map/ppermute | solution.py:16
  257.4 202.2 %all-gather.15.cloned.1.call-start = ((), (), s32[]{:S(2)}) async-start(), calls=%async_computation.3 | async-start | bytes 2703360 | tf_op jit(solution)/shard_map/all_gather | solution.py:123
  274.5 1.3 copy-start.10
  274.5 78.2 %collective-permute-start.2 = (bf16[20,64,16]{1,2,0:T(8,128)(2,1)S(1)}, bf16[20,64,16]{1,2,0:T(8,128)(2,1)S(1)}, u32[]{:S(2)}, u32[]{:S(2)}) collective-permute-start(bf16[20,64,16]{1,2,0:T(8,128)(2,1)S(1)} %multiply_convert_fusion.27), channel_id=1, source_target_pairs={{0,32},{32,64},{64,96},{1,33},{33,65},{65,97},{2,34},{34,66},{66,9... | collective-permute-start | bytes 122888 | tf_op jit(solution)/shard_map/ppermute | solution.py:16
  275.9 189.6 %all-gather.11.cloned.1.call-start = ((), (), s32[]{:S(2)}) async-start(), calls=%async_computation.1 | async-start | bytes 2703360 | tf_op jit(solution)/shard_map/all_gather | solution.py:123
  293.8 81.7 %collective-permute-start = (bf16[20,64,16]{1,2,0:T(8,128)(2,1)S(1)}, bf16[20,64,16]{1,2,0:T(8,128)(2,1)S(1)}, u32[]{:S(2)}, u32[]{:S(2)}) collective-permute-start(bf16[20,64,16]{1,2,0:T(8,128)(2,1)S(1)} %multiply_convert_fusion.29), channel_id=1, source_target_pairs={{0,32},{32,64},{64,96},{1,33},{33,65},{65,97},{2,34},{34,66},{66,9... | collective-permute-start | bytes 122888 | tf_op jit(solution)/shard_map/ppermute | solution.py:16
  295.1 57.6 %copy-start.14 = (bf16[20,64,16]{1,2,0:T(8,128)(2,1)S(1)}, bf16[20,64,16]{1,2,0:T(8,128)(2,1)}, u32[]{:S(2)}) copy-start(bf16[20,64,16]{1,2,0:T(8,128)(2,1)} %copy.78) | copy-start | bytes 122884
  295.1 217.3 %all-gather.21.cloned.1.call-start = ((), (), s32[]{:S(2)}) async-start(), calls=%async_computation.6 | async-start | bytes 2703360 | tf_op jit(solution)/shard_map/all_gather | solution.py:123
  352.8 13.4 %copy-start.13 = (bf16[20,64,16]{1,2,0:T(8,128)(2,1)S(1)}, bf16[20,64,16]{1,2,0:T(8,128)(2,1)}, u32[]{:S(2)}) copy-start(bf16[20,64,16]{1,2,0:T(8,128)(2,1)} %copy.77) | copy-start | bytes 122884
  352.8 17.1 %copy-start.2 = (bf16[8192,1280]{0,1:T(8,128)(2,1)S(1)}, bf16[8192,1280]{0,1:T(8,128)(2,1)}, u32[]{:S(2)}) copy-start(bf16[8192,1280]{0,1:T(8,128)(2,1)} %get-tuple-element.10) | copy-start | bytes 62914564
  370.0 5.5 copy-start.12
  406.8 152.8 %all-gather.19.cloned.1.call-start = ((), (), s32[]{:S(2)}) async-start(), calls=%async_computation.5 | async-start | bytes 2703360 | tf_op jit(solution)/shard_map/all_gather | solution.py:123
  433.9 18.5 %copy-start.5 = (bf16[1,1,256,1280]{2,3,1,0:T(8,128)(2,1)S(1)}, bf16[1,1,256,1280]{2,3,1,0:T(8,128)(2,1)}, u32[]{:S(2)}) copy-start(bf16[1,1,256,1280]{2,3,1,0:T(8,128)(2,1)} %copy.56) | copy-start | bytes 1966084
  433.9 172.8 %all-gather.23.cloned.1.call-start = ((), (), s32[]{:S(2)}) async-start(), calls=%async_computation.7 | async-start | bytes 2703360 | tf_op jit(solution)/shard_map/all_gather | solution.py:123
  459.7 52.8 %copy-start.4 = (bf16[1,1,256,1280]{2,3,1,0:T(8,128)(2,1)S(1)}, bf16[1,1,256,1280]{2,3,1,0:T(8,128)(2,1)}, u32[]{:S(2)}) copy-start(bf16[1,1,256,1280]{2,3,1,0:T(8,128)(2,1)} %copy.64) | copy-start | bytes 1966084
  606.7 10.8 %copy-start.1 = (bf16[20,64,512]{2,1,0:T(8,128)(2,1)S(1)}, bf16[20,64,512]{2,1,0:T(8,128)(2,1)}, u32[]{:S(2)}) copy-start(bf16[20,64,512]{2,1,0:T(8,128)(2,1)} %param.21) | copy-start | bytes 3932164
  (2 other events, 2.6 us)
Sparse Core Ops, SparseCore 0:
  19.3 151.5 all-gather.8
  173.0 149.8 all-gather.16
  325.1 46.4 all-gather.12
  373.6 44.8 all-gather.14
  420.5 44.9 all-gather.10
  467.5 44.8 all-gather.20
  514.6 44.8 all-gather.18
  561.8 44.8 all-gather.22
where the time goes:
time: 634 us; the launch traced here: 625 us
  waiting for transfers between devices  299 us (47%)
  matrix products  200 us (32%)
  local copies, waits for them, and re-layouts  82.4 us (13%)
  starting transfers between devices  15.3 us (2%)
  between operations  14.7 us (2%)
  other arithmetic  13.1 us (2%)
    all_gather x2, waiting for transfers between devices, side_by_side(): result = lax.all_gather(both, axis, axis=dim, tiled=True)  169 us
    all_gather x6, waiting for transfers between devices, shards(): lax.all_gather(as_sent(renewed), 'tok', axis=2, tiled=True)  130 us
    split x2, local copies, waits for them, and re-layouts, side_by_side(): jnp.split(result, [sum(widths[:k]) for k in range(1, len(widths))], axis=...  57.2 us
    dot_general x2, matrix products, gradients(): jnp.einsum('rhd,rhf->hdf', kk, d_gate, preferred_element_type=jnp.float32)  36.8 us
    dot_general x2, matrix products, gradients(): jnp.einsum('rhd,rhf->hdf', vv, hidden, preferred_element_type=jnp.float32)  33.1 us
    dot_general x2, matrix products, gradients(): jnp.einsum('rhd,rhf->hdf', kk, d_up, preferred_element_type=jnp.float32)  32 us
    dot_general x2, matrix products, gradients(): jnp.einsum('rhd,hdf->rhf', vv, down_w, preferred_element_type=jnp.float32)  26.9 us
    dot_general x2, matrix products, gradients(): jnp.einsum('rhd,hdf->rhf', kk, gate_w, preferred_element_type=jnp.float32)  18.9 us
  transfers between devices with their start and end apart: 11, of which 6 were waited for; matrix products, arithmetic and copies ran while one was open for 43% of the time, Pallas kernels for 0%

commit v1 on v0

v1 whole, which is shorter than its diff:
```python
import jax
import jax.numpy as jnp
from jax import lax
from jax.experimental import pallas as pl
from jax.experimental.pallas import tpu as pltpu
from jax.sharding import PartitionSpec as P

EPS = 1e-06
BF = jnp.bfloat16
F32 = jnp.float32

HEADS = 20
DH = 64
FH = 512
ROWS = 256
NTOK = 32
UNITS = FH // NTOK
PAIRS = HEADS // 2
EDGE = 176
MID = ROWS - EDGE
SUB = 16
TILE = 256
PER = TILE // SUB
SHARE = 2 * UNITS
IN_ROWS = 224
OUT_ROWS = EDGE + SHARE
LIST = NTOK * EDGE // SUB
UPS = [(3 * g + a, 3 * g + a + 1) for g in range(PAIRS) for a in (0, 1)]
DOWNS = [(3 * g + a + 1, 3 * g + a) for g in range(PAIRS) for a in (0, 1)]


def low_lanes(shape):
    return lax.broadcasted_iota(jnp.int32, shape, 1) < DH


def swap(x):
    return pltpu.roll(x.astype(F32), DH, 1).astype(x.dtype)


def pair_up(left, right):
    low = low_lanes(left.shape)
    return jnp.where(low, left, swap(right)), jnp.where(low, swap(left), right)


def scatter_rows(out_ref, g, first, second):
    out_ref[3 * g, 0:EDGE] = first[0:EDGE]
    out_ref[3 * g + 1, 0:MID] = first[EDGE:ROWS]
    out_ref[3 * g + 1, MID : 2 * MID] = second[0:MID]
    out_ref[3 * g + 2, 0:EDGE] = second[MID:ROWS]


def scaled_values(values_ref, rates_ref, counts_ref, stagger_ref, tick):
    offset = lax.broadcasted_iota(jnp.int32, (ROWS, HEADS), 0)
    inside = (offset - stagger_ref[...] + ROWS) & (ROWS - 1)
    scale = jnp.where(inside < counts_ref[tick], rates_ref[tick].astype(F32), 0.0).astype(BF)
    owner = lax.broadcasted_iota(jnp.int32, (HEADS, HEADS * DH), 1) // DH
    spread = (owner == lax.broadcasted_iota(jnp.int32, (HEADS, HEADS * DH), 0)).astype(F32).astype(BF)
    wide = jnp.dot(scale, spread, preferred_element_type=F32)
    return (values_ref[tick].astype(F32) * wide).astype(BF)


def eye(n):
    same = lax.broadcasted_iota(jnp.int32, (n, n), 0) == lax.broadcasted_iota(jnp.int32, (n, n), 1)
    return same.astype(F32).astype(BF)


def turned(share):
    return lax.dot_general(eye(UNITS), share, (((1,), (1,)), ((), ())), preferred_element_type=F32).astype(BF)


def pack_first(keys_ref, values_ref, rates_ref, counts_ref, stagger_ref, gate_ref, up_ref, down_ref, out_ref):
    scaled = scaled_values(values_ref, rates_ref, counts_ref, stagger_ref, 0)
    keys = keys_ref[0]
    gate, up, down = turned(gate_ref[...]), turned(up_ref[...]), turned(down_ref[...])
    zero = jnp.zeros((UNITS, 2 * DH), BF)
    out_ref[3 * PAIRS :] = jnp.zeros((NTOK - 3 * PAIRS, IN_ROWS, 2 * DH), BF)
    for g in range(PAIRS):
        lanes = slice(2 * DH * g, 2 * DH * (g + 1))
        first, second = pair_up(keys[:, lanes], scaled[:, lanes])
        scatter_rows(out_ref, g, first, second)
        shares = []
        for gu, w in zip(pair_up(gate[:, lanes], up[:, lanes]), pair_up(zero, down[:, lanes])):
            shares.append(jnp.concatenate([gu, w], axis=0))
        out_ref[3 * g, EDGE : EDGE + SHARE] = shares[0]
        out_ref[3 * g + 1, 2 * MID : 2 * MID + SHARE] = shares[0]
        out_ref[3 * g + 1, 2 * MID + SHARE : 2 * MID + 2 * SHARE] = shares[1]
        out_ref[3 * g + 2, EDGE : EDGE + SHARE] = shares[1]
        for d in (0, 2):
            out_ref[3 * g + d, EDGE + SHARE :] = jnp.zeros((IN_ROWS - EDGE - SHARE, 2 * DH), BF)


def finish_rows(out_ref):
    out_ref[3 * PAIRS :] = jnp.zeros((NTOK - 3 * PAIRS, EDGE, 2 * DH), BF)
    for g in range(PAIRS):
        out_ref[3 * g + 1, 2 * MID :] = jnp.zeros((EDGE - 2 * MID, 2 * DH), BF)


def pack_second(keys_ref, values_ref, rates_ref, counts_ref, stagger_ref, out_ref):
    scaled = scaled_values(values_ref, rates_ref, counts_ref, stagger_ref, 1)
    keys = keys_ref[1]
    finish_rows(out_ref)
    for g in range(PAIRS):
        lanes = slice(2 * DH * g, 2 * DH * (g + 1))
        scatter_rows(out_ref, g, *pair_up(keys[:, lanes], scaled[:, lanes]))


def pack_queries(queries_ref, out_ref):
    finish_rows(out_ref)
    for g in range(PAIRS):
        lanes = slice(2 * DH * g, 2 * DH * (g + 1))
        scatter_rows(out_ref, g, *pair_up(queries_ref[0, :, lanes], queries_ref[1, :, lanes]))


def whole_weights(role_ref, rows_ref, out_ref):
    role = role_ref[0]

    def of(start):
        gu = jnp.concatenate([rows_ref[s, pl.ds(start, UNITS)] for s in range(NTOK)], axis=0)
        w = jnp.concatenate([rows_ref[s, pl.ds(start + UNITS, UNITS)] for s in range(NTOK)], axis=0)
        gu = gu.astype(F32).T.astype(BF)
        w = w.astype(F32).T.astype(BF)
        return jnp.concatenate([gu[:DH], gu[DH:], w[DH:]], axis=1)

    start = pl.multiple_of(jnp.where(role == 1, 2 * MID, EDGE), SUB)
    out_ref[0] = of(start)
    start = pl.multiple_of(jnp.where(role == 1, 2 * MID + SHARE, EDGE), SUB)
    out_ref[1] = of(start)


def slot_bounds(role, slot):
    if slot == 0:
        return 0, jnp.where(role == 0, EDGE // SUB, jnp.where(role == 1, MID // SUB, 0))
    return (
        jnp.where(role == 1, MID // SUB, 0),
        jnp.where(role == 2, EDGE // SUB, jnp.where(role == 1, MID // SUB, 0)),
    )


def fill_list(list_ref, role, slot):
    begin, blocks = slot_bounds(role, slot)

    def per_shard(s, n):
        def per_block(j, n):
            list_ref[n] = s * 16 + begin + j
            return n + 1

        return lax.fori_loop(0, blocks, per_block, n)

    count = lax.fori_loop(0, NTOK, per_shard, jnp.int32(0))

    def pad(j, c):
        list_ref[count + j] = 0
        return c

    lax.fori_loop(0, PER, pad, 0)
    return count


def block_at(ref, entry):
    return ref[entry // 16, pl.ds(pl.multiple_of((entry % 16) * SUB, SUB), SUB)]


def gradient(role_ref, rows_ref, weights_ref, own_ref, up_ref, down_ref, stack, acc, list_ref):
    role = role_ref[0]
    zero = jnp.zeros((DH, FH), BF)
    for slot in range(2):
        w = weights_ref[slot]
        half = (w[:, :FH].astype(F32) * 0.5).astype(BF)
        stack[:DH] = jnp.concatenate([half, w[:, FH : 2 * FH], zero], axis=1)
        stack[DH:] = jnp.concatenate([zero, zero, w[:, 2 * FH :]], axis=1)
        acc[...] = jnp.zeros((DH, 3 * FH), F32)
        count = fill_list(list_ref, role, slot)

        def step(i, c):
            base = i * PER
            kv = jnp.concatenate([block_at(rows_ref, list_ref[base + j]) for j in range(PER)], axis=0)
            row = lax.broadcasted_iota(jnp.int32, (TILE, 2 * DH), 0)
            kv = jnp.where(row < (count - base) * SUB, kv.astype(F32), 0.0).astype(BF)
            turn = kv.astype(F32).T.astype(BF)
            k_t, v_t = turn[:DH], turn[DH:]
            width = 256
            for f in range(0, FH, width):
                half_gate = jnp.dot(kv, stack[:, f : f + width], preferred_element_type=F32)
                up = jnp.dot(kv, stack[:, FH + f : FH + f + width], preferred_element_type=F32)
                back = jnp.dot(kv, stack[:, 2 * FH + f : 2 * FH + f + width], preferred_element_type=F32)
                twice = jnp.tanh(half_gate) + 1.0
                act = half_gate * twice
                sig = 0.5 * twice
                slope = sig + act * (1.0 - sig)
                hidden = (act * up).astype(BF)
                d_gate = (back * up * slope).astype(BF)
                d_up = (back * act).astype(BF)
                acc[:, f : f + width] += jnp.dot(k_t, d_gate, preferred_element_type=F32)
                acc[:, FH + f : FH + f + width] += jnp.dot(k_t, d_up, preferred_element_type=F32)
                acc[:, 2 * FH + f : 2 * FH + f + width] += jnp.dot(v_t, hidden, preferred_element_type=F32)
            return c

        lax.fori_loop(0, (count + PER - 1) // PER, step, 0)
        own_ref[slot] = acc[...].astype(BF)
    up_ref[...] = own_ref[jnp.where(role == 0, 0, 1)]
    down_ref[...] = own_ref[jnp.where(role == 1, 0, 1)]


def renew(role_ref, weights_ref, own_ref, below_ref, above_ref, out_ref):
    role = role_ref[0]
    below, above = below_ref[...].astype(F32), above_ref[...].astype(F32)
    others = (jnp.where(role == 0, above, below), jnp.where(role == 1, above, below))
    for slot in range(2):
        base = weights_ref[slot].astype(F32)
        moved = base + (own_ref[slot].astype(F32) + others[slot])
        before = jnp.sum(base * base, axis=0, keepdims=True) + EPS
        after = jnp.sum(moved * moved, axis=0, keepdims=True) + EPS
        out_ref[slot] = (moved * (jnp.sqrt(before) / jnp.sqrt(after))).astype(BF)


def respond(tick):
    def kernel(role_ref, rows_ref, weights_ref, *refs):
        if tick == 0:
            out_ref, stack, list_ref = refs
        else:
            prev_ref, out_ref, stack, list_ref = refs
        role = role_ref[0]
        zero = jnp.zeros((DH, 2 * FH), BF)
        at = slice(0, DH) if tick == 0 else slice(DH, 2 * DH)
        off = slice(DH, 2 * DH) if tick == 0 else slice(0, DH)
        if tick == 0:
            out_ref[...] = jnp.zeros(out_ref.shape, BF)
        else:
            for s in range(NTOK):
                out_ref[s, 2 * MID : EDGE] = jnp.zeros((EDGE - 2 * MID, 2 * DH), BF)
        for slot in range(2):
            w = weights_ref[slot]
            half = (w[:, :FH].astype(F32) * 0.5).astype(BF)
            stack[at] = jnp.concatenate([half, w[:, FH : 2 * FH]], axis=1)
            stack[off] = zero
            nothing = jnp.zeros((DH, FH), F32)
            down = w[:, 2 * FH :].astype(F32)
            down = jnp.concatenate([down, nothing] if tick == 0 else [nothing, down], axis=0).T.astype(BF)
            count = fill_list(list_ref, role, slot)

            def step(i, c):
                base = i * PER
                q = jnp.concatenate([block_at(rows_ref, list_ref[base + j]) for j in range(PER)], axis=0)
                total = None
                width = 256
                for f in range(0, FH, width):
                    half_gate = jnp.dot(q, stack[:, f : f + width], preferred_element_type=F32)
                    up = jnp.dot(q, stack[:, FH + f : FH + f + width], preferred_element_type=F32)
                    hidden = (half_gate * (jnp.tanh(half_gate) + 1.0) * up).astype(BF)
                    part = jnp.dot(hidden, down[f : f + width], preferred_element_type=F32)
                    total = part if total is None else total + part
                answer = total.astype(BF)
                for j in range(PER):
                    entry = list_ref[base + j]
                    piece = answer[j * SUB : (j + 1) * SUB]
                    if tick == 1:
                        piece = jnp.where(low_lanes(piece.shape), block_at(prev_ref, entry), piece)
                    out_ref[entry // 16, pl.ds(pl.multiple_of((entry % 16) * SUB, SUB), SUB)] = piece
                return c

            lax.fori_loop(0, count // PER, step, 0)
        if tick == 1:
            w = jnp.where(role == 0, weights_ref[0].astype(F32), weights_ref[1].astype(F32))
            gu = jnp.concatenate([w[:, :FH], w[:, FH : 2 * FH]], axis=0).T.astype(BF)
            dn = jnp.concatenate([jnp.zeros((DH, FH), F32), w[:, 2 * FH :]], axis=0).T.astype(BF)
            for s in range(NTOK):
                out_ref[s, EDGE : EDGE + UNITS] = gu[s * UNITS : (s + 1) * UNITS]
                out_ref[s, EDGE + UNITS :] = dn[s * UNITS : (s + 1) * UNITS]

    return kernel


def unpack(rows_ref, answers_ref, gate_ref, up_ref, down_ref):
    gates, ups, downs = [], [], []
    for g in range(PAIRS):
        lanes = slice(2 * DH * g, 2 * DH * (g + 1))
        first = jnp.concatenate([rows_ref[3 * g, 0:EDGE], rows_ref[3 * g + 1, 0:MID]], axis=0)
        second = jnp.concatenate([rows_ref[3 * g + 1, MID : 2 * MID], rows_ref[3 * g + 2, 0:EDGE]], axis=0)
        tick0, tick1 = pair_up(first, second)
        answers_ref[0, :, lanes] = tick0
        answers_ref[1, :, lanes] = tick1
        one, two = rows_ref[3 * g, EDGE:], rows_ref[3 * g + 2, EDGE:]
        gate, up = pair_up(one[:UNITS], two[:UNITS])
        _, down = pair_up(one[UNITS:], two[UNITS:])
        gates.append(gate)
        ups.append(up)
        downs.append(down)
    for ref, parts in ((gate_ref, gates), (up_ref, ups), (down_ref, downs)):
        whole = jnp.concatenate(parts, axis=1)
        ref[...] = lax.dot_general(whole, eye(UNITS), (((0,), (0,)), ((), ())), preferred_element_type=F32).astype(BF)


def call(kernel, name, outs, args, scalars=0, scratch=()):
    spec = lambda: pl.BlockSpec(memory_space=pltpu.VMEM)
    many = isinstance(outs, (tuple, list))
    return pl.pallas_call(
        kernel,
        name=name,
        out_shape=outs,
        in_specs=[pl.BlockSpec(memory_space=pltpu.SMEM)] * scalars + [spec() for _ in args[scalars:]],
        out_specs=tuple(spec() for _ in outs) if many else spec(),
        scratch_shapes=list(scratch),
        compiler_params=pltpu.CompilerParams(vmem_limit_bytes=56 * 1024 * 1024),
    )(*args)


def shape(*dims):
    return jax.ShapeDtypeStruct(dims, BF)


def exchange(rows):
    result = lax.all_to_all(rows.reshape(-1, 2 * DH), "tok", split_axis=0, concat_axis=0, tiled=True)
    return result.reshape(rows.shape)


def shards(keys, values, queries, rates, counts, stagger, gate_in, up_in, down_in, entry_gate, entry_up, entry_down):
    me = lax.axis_index("tok")
    role = jnp.where(me < 3 * PAIRS, me % 3, 3).astype(jnp.int32)[None]
    pair = jnp.minimum(me // 3, PAIRS - 1)
    keys, values, queries, rates, counts = (a[0] for a in (keys, values, queries, rates, counts))
    stagger = stagger[None, :]
    shares = [w[0].reshape(HEADS * DH, UNITS) for w in (gate_in, up_in, down_in)]

    packed = call(
        pack_first,
        "pack_first",
        shape(NTOK, IN_ROWS, 2 * DH),
        (keys, values, rates, counts, stagger, *shares),
    )
    rows0 = exchange(packed)
    rows1 = exchange(
        call(pack_second, "pack_second", shape(NTOK, EDGE, 2 * DH), (keys, values, rates, counts, stagger))
    )
    rows_q = exchange(call(pack_queries, "pack_queries", shape(NTOK, EDGE, 2 * DH), (queries,)))
    entries = jnp.concatenate(
        [lax.dynamic_slice_in_dim(e, 2 * pair, 2, 0) for e in (entry_gate, entry_up, entry_down)], axis=2
    )

    weight = shape(DH, 3 * FH)
    weights = shape(2, DH, 3 * FH)
    lists = pltpu.SMEM((LIST + 2 * PER,), jnp.int32)

    def tick(rows, current):
        own, up, down = call(
            gradient,
            "gradient",
            (weights, weight, weight),
            (role, rows, current),
            1,
            (pltpu.VMEM((2 * DH, 3 * FH), BF), pltpu.VMEM((DH, 3 * FH), F32), lists),
        )
        below = lax.ppermute(up, "tok", UPS)
        above = lax.ppermute(down, "tok", DOWNS)
        return call(renew, "renew", weights, (role, current, own, below, above), 1)

    current = call(whole_weights, "whole_weights", weights, (role, rows0), 1)
    first = tick(rows0, current)
    size = lax.axis_size("block")
    passed = lax.ppermute(first, "block", [(b, b + 1) for b in range(size - 1)])
    second = tick(rows1, jnp.where(lax.axis_index("block") == 0, entries, passed))

    scratch = (pltpu.VMEM((2 * DH, 2 * FH), BF), lists)
    answers0 = call(respond(0), "respond_first", shape(NTOK, EDGE, 2 * DH), (role, rows_q, first), 1, scratch)
    packed = call(
        respond(1), "respond_second", shape(NTOK, OUT_ROWS, 2 * DH), (role, rows_q, second, answers0), 1, scratch
    )
    answers, gate, up, down = call(
        unpack,
        "unpack",
        (shape(2, ROWS, HEADS * DH),) + (shape(HEADS * DH, UNITS),) * 3,
        (exchange(packed),),
    )
    return (answers[None], *(w.reshape(1, HEADS, DH, UNITS) for w in (gate, up, down)))


def solution(mesh):
    tokens = P("block", None, "tok", None)
    share = P("block", None, None, "tok")
    return jax.shard_map(
        shards,
        mesh=mesh,
        in_specs=(tokens,) * 5 + (P(),) + (share,) * 3 + (P(),) * 3,
        out_specs=(tokens, share, share, share),
        check_vma=False,
    )
```

time: 634 us -> 237 us (0.37); the launches traced: 625 us -> 236 us
  waiting for transfers between devices: 299 us -> 49 us
  matrix products: 200 us -> 0 us
  Pallas kernels: 0 us -> 97.5 us
  local copies, waits for them, and re-layouts: 82.4 us -> 14.4 us
  blocking collectives: 0 us -> 35.2 us
  starting transfers between devices: 15.3 us -> 38.6 us
  between operations: 14.7 us -> 0.82 us
  other arithmetic: 13.1 us -> 0.84 us
    all_gather x8 -> x0, waiting for transfers between devices: 299 us -> none  [the longest x2 169 us: side_by_side(): result = lax.all_gather(both, axis, axis=dim, tiled=True)]
    dot_general x16 -> x0, matrix products: 200 us -> none  [the longest x2 36.8 us: gradients(): jnp.einsum('rhd,rhf->hdf', kk, d_gate, preferred_element_type=jnp.float32)]
    pallas_call x0 -> x11, Pallas kernels: none -> 97.5 us  [call(): pl.pallas_call(kernel, name=name, out_shape=outs, in_specs=[pl.BlockSpec(...]
    split x2 -> x0, local copies, waits for them, and re-layouts: 57.2 us -> none  [side_by_side(): jnp.split(result, [sum(widths[:k]) for k in range(1, len(widths))], axis=...]
    all_to_all x0 -> x3, waiting for transfers between devices: none -> 36.3 us  [exchange(): lax.all_to_all(rows.reshape(-1, 2 * DH), 'tok', split_axis=0, concat_axis...]
    all_to_all x0 -> x1, blocking collectives: none -> 35.2 us  [exchange(): lax.all_to_all(rows.reshape(-1, 2 * DH), 'tok', split_axis=0, concat_axis...]
    all_to_all x0 -> x3, starting transfers between devices: none -> 20.7 us  [exchange(): lax.all_to_all(rows.reshape(-1, 2 * DH), 'tok', split_axis=0, concat_axis...]
    ppermute x3 -> x5, starting transfers between devices: 3.88 us -> 17.9 us  [the longest x2 12.8 us: tick(): below = lax.ppermute(up, 'tok', UPS)]
  transfers between devices with their start and end apart: 11 -> 8, of which waited for: 6 -> 5; matrix products, arithmetic and copies ran while one was open for 43% -> 2% of each run, Pallas kernels for 0% -> 30%
where the time goes in v1:
time: 237 us; the launch traced here: 236 us
  Pallas kernels  97.5 us (41%)
  waiting for transfers between devices  49 us (21%)
  starting transfers between devices  38.6 us (16%)
  blocking collectives  35.2 us (15%)
  local copies, waits for them, and re-layouts  14.4 us (6%)
    pallas_call x11, Pallas kernels, call(): pl.pallas_call(kernel, name=name, out_shape=outs, in_specs=[pl.BlockSpec(...  97.5 us
    all_to_all x3, waiting for transfers between devices, exchange(): lax.all_to_all(rows.reshape(-1, 2 * DH), 'tok', split_axis=0, concat_axis...  36.3 us
    all_to_all x1, blocking collectives, exchange(): lax.all_to_all(rows.reshape(-1, 2 * DH), 'tok', split_axis=0, concat_axis...  35.2 us
    all_to_all x3, starting transfers between devices, exchange(): lax.all_to_all(rows.reshape(-1, 2 * DH), 'tok', split_axis=0, concat_axis...  20.7 us
    unnamed x27, local copies, waits for them, and re-layouts  13.4 us
    ppermute x2, starting transfers between devices, tick(): below = lax.ppermute(up, 'tok', UPS)  12.8 us
    ppermute x1, waiting for transfers between devices, shards(): passed = lax.ppermute(first, 'block', [(b, b + 1) for b in range(size - 1)])  7.4 us
  transfers between devices with their start and end apart: 8, of which 5 were waited for; matrix products, arithmetic and copies ran while one was open for 2% of the time, Pallas kernels for 30%

profile of v1, /device:TPU:7, one launch (start us, length us, event | category | flops | bytes accessed | tf_op | source)
XLA Modules:
  0.0 236.3 jit_solution(9122936565546813094)
XLA Ops:
  2.3 3.4 %pack_second.1 = bf16[32,176,128]{2,1,0:T(8,128)(2,1)} custom-call(bf16[2,256,1280]{2,1,0:T(8,128)(2,1)} %bitcast.16, bf16[2,256,1280]{2,1,0:T(8,128)(2,1)} %bitcast.18, bf16[2,256,20]{2,1,0:T(8,128)(2,1)} %bitcast.24, s32[2,1,20]{2,1,0:T(1,128)} %bitcast.29, s32[1,20]{1,0:T(1,128)} %bitcast.31), custom_call_target="tpu_custom_call" | custom-call | tf_op jit(solution)/shard_map/pack_second/pallas_call | solution.py:296
  5.7 8.9 %all-to-all-start.2 = ((bf16[32,176,128]{2,1,0:T(8,128)(2,1)}), bf16[32,176,128]{2,1,0:T(8,128)(2,1)S(1)}, u32[]{:S(2)}, u32[]{:S(2)}) async-start(bf16[32,176,128]{2,1,0:T(8,128)(2,1)} %pack_second.1), calls=%async_computation.2 | async-start | bytes 2883584 | tf_op jit(solution)/shard_map/all_to_all | solution.py:312
  17.3 4.1 %pack_first.1 = bf16[32,224,128]{2,1,0:T(8,128)(2,1)} custom-call(bf16[2,256,1280]{2,1,0:T(8,128)(2,1)} %bitcast.17, bf16[2,256,1280]{2,1,0:T(8,128)(2,1)} %bitcast.19, bf16[2,256,20]{2,1,0:T(8,128)(2,1)} %bitcast.25, s32[2,1,20]{2,1,0:T(1,128)} %bitcast.30, s32[1,20]{1,0:T(1,128)} %bitcast.32, bf16[1280,16]{1,0:T(8,128)(2,1)} %bitcast.20, ...), custom_call_target="tpu_custom_call" | custom-call | tf_op jit(solution)/shard_map/pack_first/pallas_call | solution.py:296
  21.4 13.8 %all-to-all-done.2.rows_ref = bf16[32,176,128]{2,1,0:T(8,128)(2,1)S(1)} async-done(((bf16[32,176,128]{2,1,0:T(8,128)(2,1)}), bf16[32,176,128]{2,1,0:T(8,128)(2,1)S(1)}, u32[]{:S(2)}, u32[]{:S(2)}) %all-to-all-start.2) | async-done | bytes 1441824 | tf_op jit(solution)/shard_map/all_to_all | solution.py:312
  36.3 5.5 %all-to-all-start.1 = ((bf16[32,224,128]{2,1,0:T(8,128)(2,1)}), bf16[32,224,128]{2,1,0:T(8,128)(2,1)S(1)}, u32[]{:S(2)}, u32[]{:S(2)}) async-start(bf16[32,224,128]{2,1,0:T(8,128)(2,1)} %pack_first.1), calls=%async_computation.1 | async-start | bytes 3670016 | tf_op jit(solution)/shard_map/all_to_all | solution.py:312
  41.8 2.9 %pack_queries.1 = bf16[32,176,128]{2,1,0:T(8,128)(2,1)} custom-call(bf16[2,256,1280]{2,1,0:T(8,128)(2,1)} %bitcast.23), custom_call_target="tpu_custom_call" | custom-call | tf_op jit(solution)/shard_map/pack_queries/pallas_call | solution.py:296
  44.7 22.5 %all-to-all-done.1.rows_ref = bf16[32,224,128]{2,1,0:T(8,128)(2,1)S(1)} async-done(((bf16[32,224,128]{2,1,0:T(8,128)(2,1)}), bf16[32,224,128]{2,1,0:T(8,128)(2,1)S(1)}, u32[]{:S(2)}, u32[]{:S(2)}) %all-to-all-start.1) | async-done | bytes 1835040 | tf_op jit(solution)/shard_map/all_to_all | solution.py:312
  68.5 6.3 %all-to-all-start = ((bf16[32,176,128]{2,1,0:T(8,128)(2,1)}), bf16[32,176,128]{2,1,0:T(8,128)(2,1)}, u32[]{:S(2)}, u32[]{:S(2)}) async-start(bf16[32,176,128]{2,1,0:T(8,128)(2,1)} %pack_queries.1), calls=%async_computation | async-start | bytes 2883584 | tf_op jit(solution)/shard_map/all_to_all | solution.py:312
  74.8 2.5 %whole_weights.1.weights_ref = bf16[2,64,1536]{2,1,0:T(8,128)(2,1)} custom-call(s32[1]{0:T(128)} %bitcast.role_ref, bf16[32,224,128]{2,1,0:T(8,128)(2,1)} %copy-done.1), custom_call_target="tpu_custom_call" | custom-call | tf_op jit(solution)/shard_map/whole_weights/pallas_call | solution.py:296
  77.2 21.8 %gradient.2 = (bf16[2,64,1536]{2,1,0:T(8,128)(2,1)}, bf16[64,1536]{1,0:T(8,128)(2,1)}, bf16[64,1536]{1,0:T(8,128)(2,1)}) custom-call(s32[1]{0:T(128)} %bitcast.role_ref, bf16[32,224,128]{2,1,0:T(8,128)(2,1)} %copy-done.1, bf16[2,64,1536]{2,1,0:T(8,128)(2,1)} %whole_weights.1.weights_ref), custom_call_target="tpu_custom_call" | custom-call | tf_op jit(solution)/shard_map/gradient/pallas_call | solution.py:296
  99.0 5.6 %collective-permute-start = (bf16[64,1536]{1,0:T(8,128)(2,1)}, bf16[64,1536]{1,0:T(8,128)(2,1)S(1)}, u32[]{:S(2)}, u32[]{:S(2)}) collective-permute-start(bf16[64,1536]{1,0:T(8,128)(2,1)} %get-tuple-element.15), channel_id=1, source_target_pairs={{0,1},{1,2},{3,4},{4,5},{6,7},{7,8},{9,10},{10,11},{12,13},{13,14}... | collective-permute-start | bytes 589832 | tf_op jit(solution)/shard_map/ppermute | solution.py:352
  104.6 1.9 collective-permute-start.1
  107.5 4.3 %collective-permute-done.1.above_ref = bf16[64,1536]{1,0:T(8,128)(2,1)S(1)} collective-permute-done((bf16[64,1536]{1,0:T(8,128)(2,1)}, bf16[64,1536]{1,0:T(8,128)(2,1)S(1)}, u32[]{:S(2)}, u32[]{:S(2)}) %collective-permute-start.1) | collective-permute-done | bytes 196640 | tf_op jit(solution)/shard_map/ppermute | solution.py:353
  112.5 2.4 %renew.2.weights_ref = bf16[2,64,1536]{2,1,0:T(8,128)(2,1)} custom-call(s32[1]{0:T(128)} %bitcast.role_ref, bf16[2,64,1536]{2,1,0:T(8,128)(2,1)} %whole_weights.1.weights_ref, bf16[2,64,1536]{2,1,0:T(8,128)(2,1)} %get-tuple-element.14.own_ref, bf16[64,1536]{1,0:T(8,128)(2,1)} %copy-done.5, bf16[64,1536]{1,0:T(8,128)(2,1)} %copy-done.6), custom_call_target="tpu_custom_call" | custom-call | tf_op jit(solution)/shard_map/renew/pallas_call | solution.py:296
  117.2 7.4 %collective-permute-done.2 = bf16[2,64,1536]{2,1,0:T(8,128)(2,1)S(1)} collective-permute-done((bf16[2,64,1536]{2,1,0:T(8,128)(2,1)}, bf16[2,64,1536]{2,1,0:T(8,128)(2,1)S(1)}, u32[]{:S(2)}, u32[]{:S(2)}) %collective-permute-start.2) | collective-permute-done | bytes 393248 | tf_op jit(solution)/shard_map/ppermute | solution.py:359
  125.5 21.7 %gradient.3 = (bf16[2,64,1536]{2,1,0:T(8,128)(2,1)}, bf16[64,1536]{1,0:T(8,128)(2,1)}, bf16[64,1536]{1,0:T(8,128)(2,1)}) custom-call(s32[1]{0:T(128)} %bitcast.role_ref, bf16[32,176,128]{2,1,0:T(8,128)(2,1)} %copy-done.2, bf16[2,64,1536]{2,1,0:T(8,128)(2,1)} %maximum_select_fusion.weights_ref), custom_call_target="tpu_custom_call" | custom-call | tf_op jit(solution)/shard_map/gradient/pallas_call | solution.py:296
  147.1 7.2 %collective-permute-start.3 = (bf16[64,1536]{1,0:T(8,128)(2,1)}, bf16[64,1536]{1,0:T(8,128)(2,1)S(1)}, u32[]{:S(2)}, u32[]{:S(2)}) collective-permute-start(bf16[64,1536]{1,0:T(8,128)(2,1)} %get-tuple-element.18), channel_id=1, source_target_pairs={{0,1},{1,2},{3,4},{4,5},{6,7},{7,8},{9,10},{10,11},{12,13},{13,14}... | collective-permute-start | bytes 589832 | tf_op jit(solution)/shard_map/ppermute | solution.py:352
  154.4 1.9 collective-permute-start.4
  156.3 16.2 %respond_first.1.refs_0_ = bf16[32,176,128]{2,1,0:T(8,128)(2,1)} custom-call(s32[1]{0:T(128)} %bitcast.role_ref, bf16[32,176,128]{2,1,0:T(8,128)(2,1)} %all-to-all-done.rows_ref, bf16[2,64,1536]{2,1,0:T(8,128)(2,1)} %renew.2.weights_ref), custom_call_target="tpu_custom_call" | custom-call | tf_op jit(solution)/shard_map/respond_first/pallas_call | solution.py:296
  173.3 2.4 %renew.3.weights_ref = bf16[2,64,1536]{2,1,0:T(8,128)(2,1)} custom-call(s32[1]{0:T(128)} %bitcast.role_ref, bf16[2,64,1536]{2,1,0:T(8,128)(2,1)} %maximum_select_fusion.weights_ref, bf16[2,64,1536]{2,1,0:T(8,128)(2,1)} %get-tuple-element.17.own_ref, bf16[64,1536]{1,0:T(8,128)(2,1)} %copy-done.3, bf16[64,1536]{1,0:T(8,128)(2,1)} %copy-done.4), custom_call_target="tpu_custom_call" | custom-call | tf_op jit(solution)/shard_map/renew/pallas_call | solution.py:296
  175.7 16.6 %respond_second.1 = bf16[32,208,128]{2,1,0:T(8,128)(2,1)} custom-call(s32[1]{0:T(128)} %bitcast.role_ref, bf16[32,176,128]{2,1,0:T(8,128)(2,1)} %all-to-all-done.rows_ref, bf16[2,64,1536]{2,1,0:T(8,128)(2,1)} %renew.3.weights_ref, bf16[32,176,128]{2,1,0:T(8,128)(2,1)} %respond_first.1.refs_0_), custom_call_target="tpu_custom_call" | custom-call | tf_op jit(solution)/shard_map/respond_second/pallas_call | solution.py:296
  192.2 35.2 %all_to_all.24.rows_ref = bf16[32,208,128]{2,1,0:T(8,128)(2,1)} all-to-all(bf16[32,208,128]{2,1,0:T(8,128)(2,1)} %respond_second.1), channel_id=1, replica_groups=mesh['block'=4,'tok'=32] {'tok'}, dimensions={0} | all-to-all | bytes 3407872 | tf_op jit(solution)/shard_map/all_to_all | solution.py:312
  227.5 3.6 %unpack.1 = (bf16[2,256,1280]{2,1,0:T(8,128)(2,1)}, bf16[1280,16]{1,0:T(8,128)(2,1)}, bf16[1280,16]{1,0:T(8,128)(2,1)}, bf16[1280,16]{1,0:T(8,128)(2,1)}) custom-call(bf16[32,208,128]{2,1,0:T(8,128)(2,1)} %all_to_all.24.rows_ref), custom_call_target="tpu_custom_call" | custom-call | tf_op jit(solution)/shard_map/unpack/pallas_call | solution.py:296
  231.0 1.8 copy.22
  (34 shorter events, 15.7 us)
Async XLA Ops:
  0.6 115.6 %copy-start = (bf16[20,64,512]{2,1,0:T(8,128)(2,1)S(1)}, bf16[20,64,512]{2,1,0:T(8,128)(2,1)}, u32[]{:S(2)}) copy-start(bf16[20,64,512]{2,1,0:T(8,128)(2,1)} %param.21) | copy-start | bytes 3932164
  5.7 8.9 %copy-start.7 = (bf16[1,20,64,16]{2,3,1,0:T(8,128)(2,1)S(1)}, bf16[1,20,64,16]{2,3,1,0:T(8,128)(2,1)}, u32[]{:S(2)}) copy-start(bf16[1,20,64,16]{2,3,1,0:T(8,128)(2,1)} %param.18) | copy-start | bytes 122884
  5.7 9.8 %copy-start.8 = (bf16[1,20,64,16]{2,3,1,0:T(8,128)(2,1)S(1)}, bf16[1,20,64,16]{2,3,1,0:T(8,128)(2,1)}, u32[]{:S(2)}) copy-start(bf16[1,20,64,16]{2,3,1,0:T(8,128)(2,1)} %param.19) | copy-start | bytes 122884
  5.7 10.7 %copy-start.9 = (bf16[1,20,64,16]{2,3,1,0:T(8,128)(2,1)S(1)}, bf16[1,20,64,16]{2,3,1,0:T(8,128)(2,1)}, u32[]{:S(2)}) copy-start(bf16[1,20,64,16]{2,3,1,0:T(8,128)(2,1)} %param.20) | copy-start | bytes 122884
  5.7 29.5 %all-to-all-start.2 = ((bf16[32,176,128]{2,1,0:T(8,128)(2,1)}), bf16[32,176,128]{2,1,0:T(8,128)(2,1)S(1)}, u32[]{:S(2)}, u32[]{:S(2)}) async-start(bf16[32,176,128]{2,1,0:T(8,128)(2,1)} %pack_second.1), calls=%async_computation.2 | async-start | bytes 2883584 | tf_op jit(solution)/shard_map/all_to_all | solution.py:312
  35.2 1.2 copy-start.2
  36.3 30.9 %all-to-all-start.1 = ((bf16[32,224,128]{2,1,0:T(8,128)(2,1)}), bf16[32,224,128]{2,1,0:T(8,128)(2,1)S(1)}, u32[]{:S(2)}, u32[]{:S(2)}) async-start(bf16[32,224,128]{2,1,0:T(8,128)(2,1)} %pack_first.1), calls=%async_computation.1 | async-start | bytes 3670016 | tf_op jit(solution)/shard_map/all_to_all | solution.py:312
  67.2 1.3 copy-start.1
  68.5 87.8 %all-to-all-start = ((bf16[32,176,128]{2,1,0:T(8,128)(2,1)}), bf16[32,176,128]{2,1,0:T(8,128)(2,1)}, u32[]{:S(2)}, u32[]{:S(2)}) async-start(bf16[32,176,128]{2,1,0:T(8,128)(2,1)} %pack_queries.1), calls=%async_computation | async-start | bytes 2883584 | tf_op jit(solution)/shard_map/all_to_all | solution.py:312
  99.0 8.5 %collective-permute-start = (bf16[64,1536]{1,0:T(8,128)(2,1)}, bf16[64,1536]{1,0:T(8,128)(2,1)S(1)}, u32[]{:S(2)}, u32[]{:S(2)}) collective-permute-start(bf16[64,1536]{1,0:T(8,128)(2,1)} %get-tuple-element.15), channel_id=1, source_target_pairs={{0,1},{1,2},{3,4},{4,5},{6,7},{7,8},{9,10},{10,11},{12,13},{13,14}... | collective-permute-start | bytes 589832 | tf_op jit(solution)/shard_map/ppermute | solution.py:352
  104.6 7.2 %collective-permute-start.1 = (bf16[64,1536]{1,0:T(8,128)(2,1)}, bf16[64,1536]{1,0:T(8,128)(2,1)S(1)}, u32[]{:S(2)}, u32[]{:S(2)}) collective-permute-start(bf16[64,1536]{1,0:T(8,128)(2,1)} %get-tuple-element.16), channel_id=1, source_target_pairs={{1,0},{2,1},{4,3},{5,4},{7,6},{8,7},{10,9},{11,10},{13,12},{14,13}... | collective-permute-start | bytes 589832 | tf_op jit(solution)/shard_map/ppermute | solution.py:353
  107.5 4.3 %copy-start.5 = (bf16[64,1536]{1,0:T(8,128)(2,1)}, bf16[64,1536]{1,0:T(8,128)(2,1)S(1)}, u32[]{:S(2)}) copy-start(bf16[64,1536]{1,0:T(8,128)(2,1)S(1)} %collective-permute-done.below_ref) | copy-start | bytes 589828
  111.8 0.7 copy-start.6
  114.9 9.8 %collective-permute-start.2 = (bf16[2,64,1536]{2,1,0:T(8,128)(2,1)}, bf16[2,64,1536]{2,1,0:T(8,128)(2,1)S(1)}, u32[]{:S(2)}, u32[]{:S(2)}) collective-permute-start(bf16[2,64,1536]{2,1,0:T(8,128)(2,1)} %renew.2.weights_ref), channel_id=1, source_target_pairs={{0,32},{32,64},{64,96},{1,33},{33,65},{65,97},{2,34},{34,66},{66,9... | collective-permute-start | bytes 1179656 | tf_op jit(solution)/shard_map/ppermute | solution.py:359
  147.1 25.4 %collective-permute-start.3 = (bf16[64,1536]{1,0:T(8,128)(2,1)}, bf16[64,1536]{1,0:T(8,128)(2,1)S(1)}, u32[]{:S(2)}, u32[]{:S(2)}) collective-permute-start(bf16[64,1536]{1,0:T(8,128)(2,1)} %get-tuple-element.18), channel_id=1, source_target_pairs={{0,1},{1,2},{3,4},{4,5},{6,7},{7,8},{9,10},{10,11},{12,13},{13,14}... | collective-permute-start | bytes 589832 | tf_op jit(solution)/shard_map/ppermute | solution.py:352
  154.4 18.1 %collective-permute-start.4 = (bf16[64,1536]{1,0:T(8,128)(2,1)}, bf16[64,1536]{1,0:T(8,128)(2,1)S(1)}, u32[]{:S(2)}, u32[]{:S(2)}) collective-permute-start(bf16[64,1536]{1,0:T(8,128)(2,1)} %get-tuple-element.19), channel_id=1, source_target_pairs={{1,0},{2,1},{4,3},{5,4},{7,6},{8,7},{10,9},{11,10},{13,12},{14,13}... | collective-permute-start | bytes 589832 | tf_op jit(solution)/shard_map/ppermute | solution.py:353
  172.5 0.7 copy-start.3
  172.5 0.7 copy-start.4

commit v2 on v1

v2 whole, which is shorter than its diff:
```python
import jax
import jax.numpy as jnp
from jax import lax
from jax.experimental import pallas as pl
from jax.experimental.pallas import tpu as pltpu
from jax.sharding import PartitionSpec as P


EPS = 1e-06
BF = jnp.bfloat16
F32 = jnp.float32

HEADS = 20
DH = 64
FH = 512
ROWS = 256
NTOK = 32
UNITS = FH // NTOK
PAIRS = HEADS // 2
EDGE = 176
MID = ROWS - EDGE
SUB = 16
TILE = 512
SHARE = 2 * UNITS
IN_ROWS = 224
HALF = EDGE // 2
OUT_ROWS = 2 * HALF + SHARE
WIDTH = 256
PIECE = 256
PACKED = NTOK * EDGE + TILE
UPS = [(3 * g + a, 3 * g + a + 1) for g in range(PAIRS) for a in (0, 1)]
DOWNS = [(3 * g + a + 1, 3 * g + a) for g in range(PAIRS) for a in (0, 1)]


def low_lanes(shape):
    return lax.broadcasted_iota(jnp.int32, shape, 1) < DH


def swap(x):
    return pltpu.roll(x.astype(F32), DH, 1).astype(x.dtype)


def pair_up(left, right):
    low = low_lanes(left.shape)
    return jnp.where(low, left, swap(right)), jnp.where(low, swap(left), right)


def scatter_rows(out_ref, g, first, second):
    out_ref[3 * g, 0:EDGE] = first[0:EDGE]
    out_ref[3 * g + 1, 0:MID] = first[EDGE:ROWS]
    out_ref[3 * g + 1, MID : 2 * MID] = second[0:MID]
    out_ref[3 * g + 2, 0:EDGE] = second[MID:ROWS]


def spread_of():
    owner = lax.broadcasted_iota(jnp.int32, (HEADS, HEADS * DH), 1) // DH
    return (owner == lax.broadcasted_iota(jnp.int32, (HEADS, HEADS * DH), 0)).astype(F32).astype(BF)


def scaled_values(values, rates_ref, counts_ref, stagger_ref, tick):
    offset = lax.broadcasted_iota(jnp.int32, (1, ROWS), 1)
    scale = []
    for h in range(HEADS):
        inside = (offset - stagger_ref[h] + ROWS) & (ROWS - 1)
        scale.append(jnp.where(inside < counts_ref[tick, h], rates_ref[h, tick : tick + 1].astype(F32), 0.0))
    scale = jnp.concatenate(scale, axis=0).astype(BF)
    wide = lax.dot_general(scale, spread_of(), (((0,), (0,)), ((), ())), preferred_element_type=F32)
    return (values.astype(F32) * wide).astype(BF)


def pack_first(
    counts_ref, stagger_ref, keys_hbm, values_hbm, rates_hbm, gate_hbm, up_hbm, down_hbm, out_hbm,
    keys_ref, values_ref, rates_ref, gate_ref, up_ref, down_ref, out_ref, loads, stores,
):
    pairs = (
        (rates_hbm, rates_ref),
        (values_hbm.at[0], values_ref),
        (keys_hbm.at[0], keys_ref),
        (gate_hbm, gate_ref),
        (up_hbm, up_ref),
        (down_hbm, down_ref),
    )
    copies = [pltpu.make_async_copy(src, dst, loads.at[n]) for n, (src, dst) in enumerate(pairs)]
    for copy in copies:
        copy.start()
    out_ref[3 * PAIRS :] = jnp.zeros((NTOK - 3 * PAIRS, IN_ROWS, 2 * DH), BF)
    for g in range(PAIRS):
        for d in (0, 2):
            out_ref[3 * g + d, EDGE + SHARE :] = jnp.zeros((IN_ROWS - EDGE - SHARE, 2 * DH), BF)
    for copy in copies:
        copy.wait()
    scaled = scaled_values(values_ref[...], rates_ref, counts_ref, stagger_ref, 0)

    def share(h):
        half = (UNITS // 2, DH)
        counts = [jnp.full(half, counts_ref[t, h].astype(F32), F32) for t in range(2)]
        gu = jnp.concatenate([gate_ref[h], up_ref[h]], axis=1)
        w = jnp.concatenate([jnp.concatenate(counts, axis=0).astype(BF), down_ref[h]], axis=1)
        return jnp.concatenate([gu, w], axis=0)

    sent = []
    for g in range(PAIRS + 1):
        lo, n = 3 * g, 3 if g < PAIRS else NTOK - 3 * PAIRS
        if g < PAIRS:
            lanes = slice(2 * DH * g, 2 * DH * (g + 1))
            first, second = pair_up(keys_ref[:, lanes], scaled[:, lanes])
            scatter_rows(out_ref, g, first, second)
            shares = share(2 * g), share(2 * g + 1)
            out_ref[3 * g, EDGE : EDGE + SHARE] = shares[0]
            out_ref[3 * g + 1, 2 * MID : 2 * MID + SHARE] = shares[0]
            out_ref[3 * g + 1, 2 * MID + SHARE : 2 * MID + 2 * SHARE] = shares[1]
            out_ref[3 * g + 2, EDGE : EDGE + SHARE] = shares[1]
        sent.append(pltpu.make_async_copy(out_ref.at[pl.ds(lo, n)], out_hbm.at[pl.ds(lo, n)], stores.at[g]))
        sent[-1].start()
    for copy in sent:
        copy.wait()


def pack_queries(queries, out_ref, at):
    out_ref[3 * PAIRS :, at : at + HALF] = jnp.zeros((NTOK - 3 * PAIRS, HALF, 2 * DH), BF)
    for g in range(PAIRS):
        tile = queries[:, 2 * DH * g : 2 * DH * (g + 1)].astype(F32)
        turn = pltpu.roll(tile, DH, 1)
        low = low_lanes((HALF, 2 * DH))
        out_ref[3 * g, at : at + HALF] = jnp.where(low, tile[:HALF], turn[HALF:EDGE]).astype(BF)
        middle = jnp.where(low_lanes((MID, 2 * DH)), tile[EDGE:], tile[:MID]).astype(BF)
        out_ref[3 * g + 1, at : at + MID] = middle
        out_ref[3 * g + 1, at + MID : at + HALF] = jnp.zeros((HALF - MID, 2 * DH), BF)
        out_ref[3 * g + 2, at : at + HALF] = jnp.where(low, turn[MID : MID + HALF], tile[MID + HALF :]).astype(BF)


def pack_second(counts_ref, stagger_ref, keys_ref, values_ref, rates_ref, queries_ref, out_ref):
    scaled = scaled_values(values_ref[1], rates_ref, counts_ref, stagger_ref, 1)
    keys = keys_ref[1]
    out_ref[3 * PAIRS :, :EDGE] = jnp.zeros((NTOK - 3 * PAIRS, EDGE, 2 * DH), BF)
    for g in range(PAIRS):
        out_ref[3 * g + 1, 2 * MID : EDGE] = jnp.zeros((EDGE - 2 * MID, 2 * DH), BF)
        lanes = slice(2 * DH * g, 2 * DH * (g + 1))
        scatter_rows(out_ref, g, *pair_up(keys[:, lanes], scaled[:, lanes]))
    pack_queries(queries_ref[0], out_ref, EDGE)


def pack_third(queries_ref, out_ref):
    pack_queries(queries_ref[1], out_ref, 0)


def whole_weights(role_ref, rows_hbm, out_ref, counts_ref, rows_ref, sem):
    copy = pltpu.make_async_copy(rows_hbm.at[:, pl.ds(2 * MID, 2 * SHARE)], rows_ref, sem)
    copy.start()
    role = role_ref[0]
    copy.wait()
    for slot in range(2):
        start = pl.multiple_of(jnp.where(role == 1, slot * SHARE, EDGE - 2 * MID), SUB)
        gu = jnp.concatenate([rows_ref[s, pl.ds(start, UNITS)] for s in range(NTOK)], axis=0)
        w = jnp.concatenate([rows_ref[s, pl.ds(start + UNITS, UNITS)] for s in range(NTOK)], axis=0)
        gu = gu.astype(F32).T.astype(BF)
        w = w.astype(F32).T
        out_ref[slot] = jnp.concatenate([gu[:DH], gu[DH:], w[DH:].astype(BF)], axis=1)
        counts_ref[slot : slot + 1] = w[0:1].astype(jnp.int32)


def gradient(tick):
    def kernel(
        role_ref, counts_ref, stagger_ref, rows_hbm, weights_ref, own_ref, up_ref, down_ref,
        stack, acc, packed, steps, total_ref, rows_ref, sem,
    ):
        copy = pltpu.make_async_copy(rows_hbm.at[:, pl.ds(0, EDGE)], rows_ref, sem)
        copy.start()
        role, pair = role_ref[0], role_ref[1]
        zero = jnp.zeros((DH, FH), BF)

        def step(base, tile):
            kv = packed[pl.ds(pl.multiple_of(base, SUB), tile)]
            turn = kv.T
            k_t, v_t = turn[:DH], turn[DH:]
            piece = min(PIECE, tile)
            for f in range(0, FH, WIDTH):
                for m in range(0, tile, piece):
                    x = kv[m : m + piece]
                    half_gate = jnp.dot(x, stack[:, f : f + WIDTH], preferred_element_type=F32)
                    up = jnp.dot(x, stack[:, FH + f : FH + f + WIDTH], preferred_element_type=F32)
                    back = jnp.dot(x, stack[:, 2 * FH + f : 2 * FH + f + WIDTH], preferred_element_type=F32)
                    twice = jnp.tanh(half_gate) + 1.0
                    act = half_gate * twice
                    sig = 0.5 * twice
                    slope = sig + act * (1.0 - sig)
                    at = slice(m, m + piece)
                    steps[at, f : f + WIDTH] = (back * up * slope).astype(BF)
                    steps[at, FH + f : FH + f + WIDTH] = (back * act).astype(BF)
                    steps[at, 2 * FH + f : 2 * FH + f + WIDTH] = (act * up).astype(BF)
            for f in range(0, 3 * FH, WIDTH):
                left = k_t if f < 2 * FH else v_t
                acc[:, f : f + WIDTH] += jnp.dot(left, steps[:tile, f : f + WIDTH], preferred_element_type=F32)

        def head(slot, begin, place, blocks):
            w = weights_ref[slot]
            half = (w[:, :FH].astype(F32) * 0.5).astype(BF)
            stack[:DH] = jnp.concatenate([half, w[:, FH : 2 * FH], zero], axis=1)
            stack[DH:] = jnp.concatenate([zero, zero, w[:, 2 * FH :]], axis=1)
            acc[...] = jnp.zeros((DH, 3 * FH), F32)
            start = stagger_ref[2 * pair + slot]
            lead = start // SUB

            def from_shard(s, n):
                limit = counts_ref[slot, s * UNITS + tick * (UNITS // 2)]
                last = (start + limit - 1) // SUB
                used = ((2 << (last - lead)) - 1) << lead
                used = ((used | (used >> (ROWS // SUB))) >> (place // SUB)) * SUB
                for j in range(blocks):
                    packed[pl.ds(pl.multiple_of(n, SUB), SUB)] = rows_ref[s, pl.ds(begin + j * SUB, SUB)]
                    n = n + ((used >> j) & SUB)
                return n

            count = lax.fori_loop(0, NTOK, from_shard, jnp.int32(0))
            packed[pl.ds(pl.multiple_of(count, SUB), TILE)] = jnp.zeros((TILE, 2 * DH), BF)
            total_ref[0] = count

        def run(slot):
            count = total_ref[0]
            whole = count // TILE
            rest = count - whole * TILE
            whole = whole + jnp.where(rest > TILE // 2, 1, 0)

            def one(i, c):
                step(i * TILE, TILE)
                return c

            lax.fori_loop(0, whole, one, 0)

            @pl.when((rest > 0) & (rest <= TILE // 2))
            def _():
                step(whole * TILE, TILE // 2)

            own_ref[slot] = acc[...].astype(BF)

        copy.wait()

        def both(slot, c):
            @pl.when(role == 1)
            def _():
                head(slot, pl.multiple_of(slot * MID, SUB), jnp.where(slot == 0, EDGE, 0), MID // SUB)

            @pl.when(role != 1)
            def _():
                head(slot, 0, jnp.where(slot == 0, 0, MID), EDGE // SUB)

            run(slot)
            return c

        lax.fori_loop(jnp.where(role == 2, 1, 0), jnp.where(role == 0, 1, jnp.where(role == 3, 0, 2)), both, 0)
        up_ref[...] = own_ref[jnp.where(role == 0, 0, 1)]
        down_ref[...] = own_ref[jnp.where(role == 1, 0, 1)]

    return kernel


def renew(role_ref, weights_ref, own_ref, below_ref, above_ref, out_ref):
    role = role_ref[0]
    below, above = below_ref[...].astype(F32), above_ref[...].astype(F32)
    others = (jnp.where(role == 0, above, below), jnp.where(role == 1, above, below))
    for slot in range(2):
        base = weights_ref[slot].astype(F32)
        moved = base + (own_ref[slot].astype(F32) + others[slot])
        before = jnp.sum(base * base, axis=0, keepdims=True) + EPS
        after = jnp.sum(moved * moved, axis=0, keepdims=True) + EPS
        out_ref[slot] = (moved * (jnp.sqrt(before) / jnp.sqrt(after))).astype(BF)


def respond(tick):
    def kernel(role_ref, rows_hbm, weights_ref, *refs):
        if tick == 0:
            prev_hbm, (out_ref, stack, down, packed, hidden, loads) = None, refs
        else:
            prev_hbm, out_ref, stack, down, packed, hidden, loads = refs
        role = role_ref[0]
        first = EDGE if tick == 0 else 0
        copies = []
        for s in range(NTOK):
            target = packed.at[pl.ds(s * HALF, HALF)]
            copies.append(pltpu.make_async_copy(rows_hbm.at[s, pl.ds(first, HALF)], target, loads.at[s]))
            copies[-1].start()
        if tick == 1:
            earlier = pltpu.make_async_copy(prev_hbm, out_ref.at[:, pl.ds(0, HALF)], loads.at[NTOK])
            earlier.start()
        nothing = jnp.zeros((DH, FH), F32)
        for side in range(2):
            w = weights_ref[jnp.where(role == 2, 1, jnp.where(role == 1, side, 0))]
            half = (w[:, :FH].astype(F32) * 0.5).astype(BF)
            mine = jnp.concatenate([half, w[:, FH : 2 * FH]], axis=1)
            stack[side, side * DH : (side + 1) * DH] = mine
            stack[side, (1 - side) * DH : (2 - side) * DH] = jnp.zeros((DH, 2 * FH), BF)
            back = w[:, 2 * FH :].astype(F32)
            turn = jnp.concatenate([back, nothing] if side == 0 else [nothing, back], axis=0).T.astype(BF)
            down[side * FH : (side + 1) * FH] = turn
        for copy in copies:
            copy.wait()

        def step(i, c):
            tile = pl.ds(pl.multiple_of(i * PIECE, PIECE), PIECE)
            q = packed[tile]
            for side in range(2):
                for f in range(0, FH, WIDTH):
                    half_gate = jnp.dot(q, stack[side, :, f : f + WIDTH], preferred_element_type=F32)
                    up = jnp.dot(q, stack[side, :, FH + f : FH + f + WIDTH], preferred_element_type=F32)
                    value = half_gate * (jnp.tanh(half_gate) + 1.0) * up
                    hidden[:, side * FH + f : side * FH + f + WIDTH] = value.astype(BF)
            packed[tile] = jnp.dot(hidden[...], down[...], preferred_element_type=F32).astype(BF)
            return c

        lax.fori_loop(0, NTOK * HALF // PIECE, step, 0)
        at = tick * HALF
        for s in range(NTOK):
            out_ref[s, at : at + HALF] = packed[s * HALF : (s + 1) * HALF]
        if tick == 1:
            w = jnp.where(role == 0, weights_ref[0].astype(F32), weights_ref[1].astype(F32))
            gu = jnp.concatenate([w[:, :FH], w[:, FH : 2 * FH]], axis=0).T.astype(BF)
            dn = jnp.concatenate([w[:, 2 * FH :], nothing], axis=0).T.astype(BF)
            for s in range(NTOK):
                out_ref[s, 2 * HALF : 2 * HALF + UNITS] = gu[s * UNITS : (s + 1) * UNITS]
                out_ref[s, 2 * HALF + UNITS :] = dn[s * UNITS : (s + 1) * UNITS]
            earlier.wait()

    return kernel


def unpack(rows_ref, answers_ref, gate_ref, up_ref, down_ref):
    for g in range(PAIRS):
        lanes = slice(2 * DH * g, 2 * DH * (g + 1))
        for t in range(2):
            one, mid, two = (rows_ref[3 * g + d, t * HALF : (t + 1) * HALF].astype(F32) for d in range(3))
            first = jnp.concatenate([one, pltpu.roll(one, DH, 1), mid[:MID]], axis=0)
            second = jnp.concatenate([mid[:MID], pltpu.roll(two, DH, 1), two], axis=0)
            answers_ref[t, :, lanes] = jnp.where(low_lanes(first.shape), first, second).astype(BF)
        for h in range(2):
            share = rows_ref[3 * g + 2 * h, 2 * HALF :]
            gate_ref[2 * g + h] = share[:UNITS, :DH]
            up_ref[2 * g + h] = swap(share[:UNITS])[:, :DH]
            down_ref[2 * g + h] = share[UNITS:, :DH]


def call(kernel, outs, args, scalars=0, scratch=(), remote=(), far=False):
    places = [pltpu.SMEM if n < scalars else pltpu.HBM if n in remote else pltpu.VMEM for n in range(len(args))]
    args = [pltpu.with_memory_space_constraint(a, p) if p == pltpu.HBM else a for a, p in zip(args, places)]
    many = isinstance(outs, (tuple, list))
    out = lambda: pl.BlockSpec(memory_space=pltpu.HBM if far else pltpu.VMEM)
    if far:
        outs = pltpu.HBM(outs.shape, outs.dtype)
    return pl.pallas_call(
        kernel,
        out_shape=outs,
        in_specs=[pl.BlockSpec(memory_space=p) for p in places],
        out_specs=tuple(out() for _ in outs) if many else out(),
        scratch_shapes=list(scratch),
        compiler_params=pltpu.CompilerParams(vmem_limit_bytes=24 * 1024 * 1024),
    )(*args)


def shape(*dims):
    return jax.ShapeDtypeStruct(dims, BF)


def exchange(rows):
    result = lax.all_to_all(rows.reshape(-1, 2 * DH), "tok", split_axis=0, concat_axis=0, tiled=True)
    return result.reshape(rows.shape)


def program(keys, values, queries, rates, counts, stagger, gate_in, up_in, down_in, entry_gate, entry_up, entry_down):
    me = lax.axis_index("tok")
    pair = jnp.minimum(me // 3, PAIRS - 1)
    role = jnp.stack([jnp.where(me < 3 * PAIRS, me % 3, 3), pair]).astype(jnp.int32)
    keys, values, queries = keys[0], values[0], queries[0]
    rates = jnp.transpose(rates[0], (2, 0, 1))
    counts = counts[0, :, 0]
    shares = [jnp.transpose(w[0], (0, 2, 1)) for w in (gate_in, up_in, down_in)]
    tokens = (counts, stagger, keys, values, rates)
    scratch = [pltpu.VMEM((ROWS, HEADS * DH), BF)] * 2 + [pltpu.VMEM(rates.shape, BF)]
    scratch += [pltpu.VMEM((HEADS, UNITS, DH), BF)] * 3 + [pltpu.VMEM((NTOK, IN_ROWS, 2 * DH), BF)]
    scratch += [pltpu.SemaphoreType.DMA((6,)), pltpu.SemaphoreType.DMA((PAIRS + 1,))]
    operands = (*tokens, *shares)
    packed0 = call(pack_first, shape(NTOK, IN_ROWS, 2 * DH), operands, 2, scratch, range(2, len(operands)), True)
    rows0 = exchange(packed0)
    tokens, queries, packed0 = lax.optimization_barrier((tokens, queries, packed0))
    packed1 = call(pack_second, shape(NTOK, EDGE + HALF, 2 * DH), (*tokens, queries), 2)
    packed_q = call(pack_third, shape(NTOK, HALF, 2 * DH), (queries,))
    rows0, packed1, packed_q = lax.optimization_barrier((rows0, packed1, packed_q))
    rows1 = exchange(packed1)
    entries = jnp.concatenate(
        [lax.dynamic_slice_in_dim(e, 2 * pair, 2, 0) for e in (entry_gate, entry_up, entry_down)], axis=2
    )

    weight = shape(DH, 3 * FH)
    weights = shape(2, DH, 3 * FH)
    stacked = (pltpu.VMEM((2 * DH, 3 * FH), BF), pltpu.VMEM((DH, 3 * FH), F32))
    scratch = (*stacked, pltpu.VMEM((PACKED, 2 * DH), BF), pltpu.VMEM((TILE, 3 * FH), BF), pltpu.SMEM((1,), jnp.int32))
    scratch += (pltpu.VMEM((NTOK, EDGE, 2 * DH), BF), pltpu.SemaphoreType.DMA)

    def advance(tick, rows, current, limits):
        own, up, down = call(
            gradient(tick), (weights, weight, weight), (role, limits, stagger, rows, current), 3, scratch, (3,)
        )
        below = lax.ppermute(up, "tok", UPS)
        above = lax.ppermute(down, "tok", DOWNS)
        return call(renew, weights, (role, current, own, below, above), 1)

    current, limits = call(
        whole_weights,
        (weights, jax.ShapeDtypeStruct((2, FH), jnp.int32)),
        (role, rows0),
        1,
        (pltpu.VMEM((NTOK, 2 * SHARE, 2 * DH), BF), pltpu.SemaphoreType.DMA),
        (1,),
    )
    first = advance(0, rows0, current, limits)
    first, packed_q = lax.optimization_barrier((first, packed_q))
    rows_q = exchange(packed_q)
    size = lax.axis_size("block")
    passed = lax.ppermute(first, "block", [(b, b + 1) for b in range(size - 1)])
    second = advance(1, rows1, jnp.where(lax.axis_index("block") == 0, entries, passed), limits)

    scratch_q = (
        pltpu.VMEM((2, 2 * DH, 2 * FH), BF),
        pltpu.VMEM((2 * FH, 2 * DH), BF),
        pltpu.VMEM((NTOK * HALF, 2 * DH), BF),
        pltpu.VMEM((PIECE, 2 * FH), BF),
        pltpu.SemaphoreType.DMA((NTOK + 1,)),
    )
    answers0 = call(respond(0), shape(NTOK, HALF, 2 * DH), (role, rows1, first), 1, scratch_q, (1,))
    operands = (role, rows_q, second, answers0)
    packed = call(respond(1), shape(NTOK, OUT_ROWS, 2 * DH), operands, 1, scratch_q, (1, 3))
    answers, gate, up, down = call(
        unpack, (shape(2, ROWS, HEADS * DH),) + (shape(HEADS, UNITS, DH),) * 3, (exchange(packed),)
    )
    return (answers[None], *(jnp.transpose(w, (0, 2, 1))[None] for w in (gate, up, down)))


def solution(mesh):
    tokens = P("block", None, "tok", None)
    share = P("block", None, None, "tok")
    return jax.shard_map(
        program,
        mesh=mesh,
        in_specs=(tokens,) * 5 + (P(),) + (share,) * 3 + (P(),) * 3,
        out_specs=(tokens, share, share, share),
        check_vma=False,
    )
```

time: 237 us -> 158 us (0.67)
  the two profiles are of different devices: /device:TPU:7 before, /device:TPU:1 now
where the time goes in v2:
time: 158 us; the launch traced here: 157 us
  Pallas kernels  45.7 us (29%)
  starting transfers between devices  41.5 us (26%)
  blocking collectives  33 us (21%)
  waiting for transfers between devices  30.4 us (19%)
  local copies, waits for them, and re-layouts  5.6 us (4%)
    pallas_call x11, Pallas kernels, call(): pl.pallas_call(kernel, out_shape=outs, in_specs=[pl.BlockSpec(memory_spac...  45.7 us
    all_to_all x1, blocking collectives, exchange(): lax.all_to_all(rows.reshape(-1, 2 * DH), 'tok', split_axis=0, concat_axis...  33 us
    all_to_all x3, starting transfers between devices, exchange(): lax.all_to_all(rows.reshape(-1, 2 * DH), 'tok', split_axis=0, concat_axis...  22.9 us
    all_to_all x3, waiting for transfers between devices, exchange(): lax.all_to_all(rows.reshape(-1, 2 * DH), 'tok', split_axis=0, concat_axis...  20.6 us
    ppermute x2, starting transfers between devices, advance(): below = lax.ppermute(up, 'tok', UPS)  11.3 us
    ppermute x2, waiting for transfers between devices, advance(): below = lax.ppermute(up, 'tok', UPS)  7.8 us
    unnamed x22, local copies, waits for them, and re-layouts  4.59 us
    ppermute x2, starting transfers between devices, advance(): above = lax.ppermute(down, 'tok', DOWNS)  3.84 us
  transfers between devices with their start and end apart: 8, of which 3 were waited for; matrix products, arithmetic and copies ran while one was open for 1% of the time, Pallas kernels for 20%

profile of v2, /device:TPU:1, one launch (start us, length us, event | category | flops | bytes accessed | tf_op | source)
XLA Modules:
  0.0 157.3 jit_solution(17449678614012818523)
XLA Ops:
  2.1 3.7 %shard_map.147 = bf16[32,224,128]{2,1,0:T(8,128)(2,1)} custom-call(s32[2,20]{1,0:T(2,128)S(1)} %bitcast.36, s32[20]{0:T(128)S(1)} %copy-done.6, bf16[2,256,1280]{2,1,0:T(8,128)(2,1)} %bitcast.28, bf16[2,256,1280]{2,1,0:T(8,128)(2,1)} %bitcast.30, bf16[20,2,256]{2,1,0:T(2,128)(2,1)} %bitcast.34, bf16[20,16,64]{2,1,0:T(8,128)(2,1)} %bitcast.38, ...), custom_call_target="tpu_custom_call" | custom-call | tf_op jit(solution)/shard_map/pallas_call | solution.py:348
  5.8 9.8 %all-to-all-start = ((bf16[32,224,128]{2,1,0:T(8,128)(2,1)}), bf16[32,224,128]{2,1,0:T(8,128)(2,1)}, u32[]{:S(2)}, u32[]{:S(2)}) async-start(bf16[32,224,128]{2,1,0:T(8,128)(2,1)} %shard_map.147), calls=%async_computation | async-start | bytes 3670016 | tf_op jit(solution)/shard_map/all_to_all | solution.py:363
  15.6 1.4 copy-done.3
  17.1 1.0 shard_map.149
  18.1 2.7 %shard_map.148 = bf16[32,264,128]{2,1,0:T(8,128)(2,1)} custom-call(s32[2,20]{1,0:T(2,128)S(1)} %bitcast.37, s32[20]{0:T(128)S(1)} %copy-done.7, bf16[2,256,1280]{2,1,0:T(8,128)(2,1)S(1)} %bitcast.29, bf16[2,256,1280]{2,1,0:T(8,128)(2,1)S(1)} %bitcast.31, bf16[20,2,256]{2,1,0:T(2,128)(2,1)S(1)} %bitcast.35, bf16[2,256,1280]{2,1,0:T(8,128)(2,1)S(1)} %bitcast.33), custom_call_target="tpu_custom_call" | custom-call | tf_op jit(solution)/shard_map/pallas_call | solution.py:348
  20.8 20.6 %all-to-all-done.rows_hbm = bf16[32,224,128]{2,1,0:T(8,128)(2,1)} async-done(((bf16[32,224,128]{2,1,0:T(8,128)(2,1)}), bf16[32,224,128]{2,1,0:T(8,128)(2,1)}, u32[]{:S(2)}, u32[]{:S(2)}) %all-to-all-start) | async-done | bytes 1835040 | tf_op jit(solution)/shard_map/all_to_all | solution.py:363
  41.4 5.9 %all-to-all-start.2 = ((bf16[32,264,128]{2,1,0:T(8,128)(2,1)}), bf16[32,264,128]{2,1,0:T(8,128)(2,1)}, u32[]{:S(2)}, u32[]{:S(2)}) async-start(bf16[32,264,128]{2,1,0:T(8,128)(2,1)} %shard_map.148), calls=%async_computation.2 | async-start | bytes 4325376 | tf_op jit(solution)/shard_map/all_to_all | solution.py:363
  47.4 1.8 %shard_map.150 = (bf16[2,64,1536]{2,1,0:T(8,128)(2,1)S(1)}, s32[2,512]{1,0:T(2,128)S(1)}) custom-call(s32[2]{0:T(128)S(1)} %pad_add_fusion.role_ref, bf16[32,224,128]{2,1,0:T(8,128)(2,1)} %all-to-all-done.rows_hbm), custom_call_target="tpu_custom_call" | custom-call | tf_op jit(solution)/shard_map/pallas_call | solution.py:348
  49.2 8.4 %shard_map.151 = (bf16[2,64,1536]{2,1,0:T(8,128)(2,1)S(1)}, bf16[64,1536]{1,0:T(8,128)(2,1)S(1)}, bf16[64,1536]{1,0:T(8,128)(2,1)S(1)}) custom-call(s32[2]{0:T(128)S(1)} %pad_add_fusion.role_ref, s32[2,512]{1,0:T(2,128)S(1)} %get-tuple-element.35.counts_ref, s32[20]{0:T(128)S(1)} %copy-done.7, bf16[32,224,128]{2,1,0:T(8,128)(2,1)} %all-to-all-done.rows_hbm, ...), custom_call_target="tpu_custom_call" | custom-call | tf_op jit(solution)/shard_map/pallas_call | solution.py:348
  57.7 5.8 %collective-permute-start = (bf16[64,1536]{1,0:T(8,128)(2,1)S(1)}, bf16[64,1536]{1,0:T(8,128)(2,1)S(1)}, u32[]{:S(2)}, u32[]{:S(2)}) collective-permute-start(bf16[64,1536]{1,0:T(8,128)(2,1)S(1)} %get-tuple-element.37), channel_id=1, source_target_pairs={{0,1},{1,2},{3,4},{4,5},{6,7},{7,8},{9,10},{10,11},{12,13},{13,14}... | collective-permute-start | bytes 589832 | tf_op jit(solution)/shard_map/ppermute | solution.py:401
  63.5 1.9 %collective-permute-start.1 = (bf16[64,1536]{1,0:T(8,128)(2,1)S(1)}, bf16[64,1536]{1,0:T(8,128)(2,1)S(1)}, u32[]{:S(2)}, u32[]{:S(2)}) collective-permute-start(bf16[64,1536]{1,0:T(8,128)(2,1)S(1)} %get-tuple-element.38), channel_id=1, source_target_pairs={{1,0},{2,1},{4,3},{5,4},{7,6},{8,7},{10,9},{11,10},{13,12},{14,13}... | collective-permute-start | bytes 589832 | tf_op jit(solution)/shard_map/ppermute | solution.py:402
  65.4 7.8 %collective-permute-done.below_ref = bf16[64,1536]{1,0:T(8,128)(2,1)S(1)} collective-permute-done((bf16[64,1536]{1,0:T(8,128)(2,1)S(1)}, bf16[64,1536]{1,0:T(8,128)(2,1)S(1)}, u32[]{:S(2)}, u32[]{:S(2)}) %collective-permute-start) | collective-permute-done | bytes 196640 | tf_op jit(solution)/shard_map/ppermute | solution.py:401
  73.2 2.1 %collective-permute-done.1.above_ref = bf16[64,1536]{1,0:T(8,128)(2,1)S(1)} collective-permute-done((bf16[64,1536]{1,0:T(8,128)(2,1)S(1)}, bf16[64,1536]{1,0:T(8,128)(2,1)S(1)}, u32[]{:S(2)}, u32[]{:S(2)}) %collective-permute-start.1) | collective-permute-done | bytes 196640 | tf_op jit(solution)/shard_map/ppermute | solution.py:402
  76.3 3.4 %collective-permute-start.2 = (bf16[2,64,1536]{2,1,0:T(8,128)(2,1)S(1)}, bf16[2,64,1536]{2,1,0:T(8,128)(2,1)S(1)}, u32[]{:S(2)}, u32[]{:S(2)}) collective-permute-start(bf16[2,64,1536]{2,1,0:T(8,128)(2,1)S(1)} %shard_map.152.weights_ref), channel_id=1, source_target_pairs={{0,32},{32,64},{64,96},{1,33},{33,65},{65,97},{2,34},{34,66},{66,9... | collective-permute-start | bytes 1179656 | tf_op jit(solution)/shard_map/ppermute | solution.py:417
  79.7 1.0 constant_dynamic-slice_fusion
  80.7 7.2 %all-to-all-start.1 = ((bf16[32,88,128]{2,1,0:T(8,128)(2,1)}), bf16[32,88,128]{2,1,0:T(8,128)(2,1)S(1)}, u32[]{:S(2)}, u32[]{:S(2)}) async-start(bf16[32,88,128]{2,1,0:T(8,128)(2,1)} %shard_map.149), calls=%async_computation.1 | async-start | bytes 1441792 | tf_op jit(solution)/shard_map/all_to_all | solution.py:363
  88.1 8.2 %shard_map.153 = (bf16[2,64,1536]{2,1,0:T(8,128)(2,1)S(1)}, bf16[64,1536]{1,0:T(8,128)(2,1)S(1)}, bf16[64,1536]{1,0:T(8,128)(2,1)S(1)}) custom-call(s32[2]{0:T(128)S(1)} %pad_add_fusion.role_ref, s32[2,512]{1,0:T(2,128)S(1)} %get-tuple-element.35.counts_ref, s32[20]{0:T(128)S(1)} %copy-done.7, bf16[32,264,128]{2,1,0:T(8,128)(2,1)} %all-to-all-done.2.rows_hbm, ...), custom_call_target="tpu_custom_call" | custom-call | tf_op jit(solution)/shard_map/pallas_call | solution.py:348
  96.3 5.4 %collective-permute-start.3 = (bf16[64,1536]{1,0:T(8,128)(2,1)S(1)}, bf16[64,1536]{1,0:T(8,128)(2,1)S(1)}, u32[]{:S(2)}, u32[]{:S(2)}) collective-permute-start(bf16[64,1536]{1,0:T(8,128)(2,1)S(1)} %get-tuple-element.44), channel_id=1, source_target_pairs={{0,1},{1,2},{3,4},{4,5},{6,7},{7,8},{9,10},{10,11},{12,13},{13,14}... | collective-permute-start | bytes 589832 | tf_op jit(solution)/shard_map/ppermute | solution.py:401
  101.8 1.9 %collective-permute-start.4 = (bf16[64,1536]{1,0:T(8,128)(2,1)S(1)}, bf16[64,1536]{1,0:T(8,128)(2,1)S(1)}, u32[]{:S(2)}, u32[]{:S(2)}) collective-permute-start(bf16[64,1536]{1,0:T(8,128)(2,1)S(1)} %get-tuple-element.45), channel_id=1, source_target_pairs={{1,0},{2,1},{4,3},{5,4},{7,6},{8,7},{10,9},{11,10},{13,12},{14,13}... | collective-permute-start | bytes 589832 | tf_op jit(solution)/shard_map/ppermute | solution.py:402
  103.7 8.2 %shard_map.155.refs_0_ = bf16[32,88,128]{2,1,0:T(8,128)(2,1)S(1)} custom-call(s32[2]{0:T(128)S(1)} %pad_add_fusion.role_ref, bf16[32,264,128]{2,1,0:T(8,128)(2,1)} %all-to-all-done.2.rows_hbm, bf16[2,64,1536]{2,1,0:T(8,128)(2,1)S(1)} %shard_map.152.weights_ref), custom_call_target="tpu_custom_call" | custom-call | tf_op jit(solution)/shard_map/pallas_call | solution.py:348
  112.7 0.9 shard_map.154.weights_ref
  114.6 8.2 %shard_map.156 = bf16[32,208,128]{2,1,0:T(8,128)(2,1)S(1)} custom-call(s32[2]{0:T(128)S(1)} %pad_add_fusion.role_ref, bf16[32,88,128]{2,1,0:T(8,128)(2,1)} %copy-done.10, bf16[2,64,1536]{2,1,0:T(8,128)(2,1)S(1)} %shard_map.154.weights_ref, bf16[32,88,128]{2,1,0:T(8,128)(2,1)} %copy-done.4), custom_call_target="tpu_custom_call" | custom-call | tf_op jit(solution)/shard_map/pallas_call | solution.py:348
  122.8 33.0 %all_to_all.24.rows_ref = bf16[32,208,128]{2,1,0:T(8,128)(2,1)S(1)} all-to-all(bf16[32,208,128]{2,1,0:T(8,128)(2,1)S(1)} %shard_map.156), channel_id=1, replica_groups=mesh['block'=4,'tok'=32] {'tok'}, dimensions={0} | all-to-all | bytes 3407872 | tf_op jit(solution)/shard_map/all_to_all | solution.py:363
  155.9 1.5 shard_map.157
  (30 shorter events, 4.3 us)
Async XLA Ops:
  0.6 87.3 %copy-start = (bf16[20,64,512]{2,1,0:T(8,128)(2,1)S(1)}, bf16[20,64,512]{2,1,0:T(8,128)(2,1)}, u32[]{:S(2)}) copy-start(bf16[20,64,512]{2,1,0:T(8,128)(2,1)} %param.21) | copy-start | bytes 3932164
  0.6 0.8 copy-start.6
  1.4 0.7 copy-start.8
  5.8 12.3 %copy-start.2 = (bf16[1,2,256,1280]{3,2,1,0:T(8,128)(2,1)S(1)}, bf16[1,2,256,1280]{3,2,1,0:T(8,128)(2,1)}, u32[]{:S(2)}) copy-start(bf16[1,2,256,1280]{3,2,1,0:T(8,128)(2,1)} %param.13) | copy-start | bytes 3932164
  5.8 35.5 %all-to-all-start = ((bf16[32,224,128]{2,1,0:T(8,128)(2,1)}), bf16[32,224,128]{2,1,0:T(8,128)(2,1)}, u32[]{:S(2)}, u32[]{:S(2)}) async-start(bf16[32,224,128]{2,1,0:T(8,128)(2,1)} %shard_map.147), calls=%async_computation | async-start | bytes 3670016 | tf_op jit(solution)/shard_map/all_to_all | solution.py:363
  15.6 2.5 %copy-start.1 = (bf16[1,2,256,1280]{3,2,1,0:T(8,128)(2,1)S(1)}, bf16[1,2,256,1280]{3,2,1,0:T(8,128)(2,1)}, u32[]{:S(2)}) copy-start(bf16[1,2,256,1280]{3,2,1,0:T(8,128)(2,1)} %param.12) | copy-start | bytes 3932164
  15.6 1.4 copy-start.3
  17.1 1.0 copy-start.5
  17.1 1.0 copy-start.7
  17.1 1.1 copy-start.9
  41.4 39.3 %all-to-all-start.2 = ((bf16[32,264,128]{2,1,0:T(8,128)(2,1)}), bf16[32,264,128]{2,1,0:T(8,128)(2,1)}, u32[]{:S(2)}, u32[]{:S(2)}) async-start(bf16[32,264,128]{2,1,0:T(8,128)(2,1)} %shard_map.148), calls=%async_computation.2 | async-start | bytes 4325376 | tf_op jit(solution)/shard_map/all_to_all | solution.py:363
  57.7 15.6 %collective-permute-start = (bf16[64,1536]{1,0:T(8,128)(2,1)S(1)}, bf16[64,1536]{1,0:T(8,128)(2,1)S(1)}, u32[]{:S(2)}, u32[]{:S(2)}) collective-permute-start(bf16[64,1536]{1,0:T(8,128)(2,1)S(1)} %get-tuple-element.37), channel_id=1, source_target_pairs={{0,1},{1,2},{3,4},{4,5},{6,7},{7,8},{9,10},{10,11},{12,13},{13,14}... | collective-permute-start | bytes 589832 | tf_op jit(solution)/shard_map/ppermute | solution.py:401
  63.5 11.8 %collective-permute-start.1 = (bf16[64,1536]{1,0:T(8,128)(2,1)S(1)}, bf16[64,1536]{1,0:T(8,128)(2,1)S(1)}, u32[]{:S(2)}, u32[]{:S(2)}) collective-permute-start(bf16[64,1536]{1,0:T(8,128)(2,1)S(1)} %get-tuple-element.38), channel_id=1, source_target_pairs={{1,0},{2,1},{4,3},{5,4},{7,6},{8,7},{10,9},{11,10},{13,12},{14,13}... | collective-permute-start | bytes 589832 | tf_op jit(solution)/shard_map/ppermute | solution.py:402
  76.3 11.7 %collective-permute-start.2 = (bf16[2,64,1536]{2,1,0:T(8,128)(2,1)S(1)}, bf16[2,64,1536]{2,1,0:T(8,128)(2,1)S(1)}, u32[]{:S(2)}, u32[]{:S(2)}) collective-permute-start(bf16[2,64,1536]{2,1,0:T(8,128)(2,1)S(1)} %shard_map.152.weights_ref), channel_id=1, source_target_pairs={{0,32},{32,64},{64,96},{1,33},{33,65},{65,97},{2,34},{34,66},{66,9... | collective-permute-start | bytes 1179656 | tf_op jit(solution)/shard_map/ppermute | solution.py:417
  80.7 33.0 %all-to-all-start.1 = ((bf16[32,88,128]{2,1,0:T(8,128)(2,1)}), bf16[32,88,128]{2,1,0:T(8,128)(2,1)S(1)}, u32[]{:S(2)}, u32[]{:S(2)}) async-start(bf16[32,88,128]{2,1,0:T(8,128)(2,1)} %shard_map.149), calls=%async_computation.1 | async-start | bytes 1441792 | tf_op jit(solution)/shard_map/all_to_all | solution.py:363
  96.3 16.4 %collective-permute-start.3 = (bf16[64,1536]{1,0:T(8,128)(2,1)S(1)}, bf16[64,1536]{1,0:T(8,128)(2,1)S(1)}, u32[]{:S(2)}, u32[]{:S(2)}) collective-permute-start(bf16[64,1536]{1,0:T(8,128)(2,1)S(1)} %get-tuple-element.44), channel_id=1, source_target_pairs={{0,1},{1,2},{3,4},{4,5},{6,7},{7,8},{9,10},{10,11},{12,13},{13,14}... | collective-permute-start | bytes 589832 | tf_op jit(solution)/shard_map/ppermute | solution.py:401
  101.8 11.0 %collective-permute-start.4 = (bf16[64,1536]{1,0:T(8,128)(2,1)S(1)}, bf16[64,1536]{1,0:T(8,128)(2,1)S(1)}, u32[]{:S(2)}, u32[]{:S(2)}) collective-permute-start(bf16[64,1536]{1,0:T(8,128)(2,1)S(1)} %get-tuple-element.45), channel_id=1, source_target_pairs={{1,0},{2,1},{4,3},{5,4},{7,6},{8,7},{10,9},{11,10},{13,12},{14,13}... | collective-permute-start | bytes 589832 | tf_op jit(solution)/shard_map/ppermute | solution.py:402
  111.9 0.9 copy-start.4
  113.7 0.9 copy-start.10

commit v3 on v2

--- a/solution.py
+++ b/solution.py
@@ -4,7 +4,6 @@
 from jax.experimental import pallas as pl
 from jax.experimental.pallas import tpu as pltpu
 from jax.sharding import PartitionSpec as P
-
 
 EPS = 1e-06
 BF = jnp.bfloat16
@@ -21,8 +20,11 @@
 MID = ROWS - EDGE
 SUB = 16
 TILE = 512
+PER = TILE // SUB
 SHARE = 2 * UNITS
 IN_ROWS = 224
+MID_BLOCKS = (1, 4, 7, 10, 13)
+EDGE_BLOCKS = tuple(b for b in range(ROWS // SUB) if b not in MID_BLOCKS)
 HALF = EDGE // 2
 OUT_ROWS = 2 * HALF + SHARE
 WIDTH = 256
@@ -46,10 +48,14 @@
 
 
 def scatter_rows(out_ref, g, first, second):
-    out_ref[3 * g, 0:EDGE] = first[0:EDGE]
-    out_ref[3 * g + 1, 0:MID] = first[EDGE:ROWS]
-    out_ref[3 * g + 1, MID : 2 * MID] = second[0:MID]
-    out_ref[3 * g + 2, 0:EDGE] = second[MID:ROWS]
+    for j, b in enumerate(EDGE_BLOCKS):
+        to, of = slice(j * SUB, (j + 1) * SUB), slice(b * SUB, (b + 1) * SUB)
+        out_ref[3 * g, to] = first[of]
+        out_ref[3 * g + 2, to] = second[of]
+    for j, b in enumerate(MID_BLOCKS):
+        of = slice(b * SUB, (b + 1) * SUB)
+        out_ref[3 * g + 1, j * SUB : (j + 1) * SUB] = first[of]
+        out_ref[3 * g + 1, MID + j * SUB : MID + (j + 1) * SUB] = second[of]
 
 
 def spread_of():
@@ -137,11 +143,8 @@
         out_ref[3 * g + 1, 2 * MID : EDGE] = jnp.zeros((EDGE - 2 * MID, 2 * DH), BF)
         lanes = slice(2 * DH * g, 2 * DH * (g + 1))
         scatter_rows(out_ref, g, *pair_up(keys[:, lanes], scaled[:, lanes]))
-    pack_queries(queries_ref[0], out_ref, EDGE)
-
-
-def pack_third(queries_ref, out_ref):
-    pack_queries(queries_ref[1], out_ref, 0)
+    for t in range(2):
+        pack_queries(queries_ref[t], out_ref, EDGE + t * HALF)
 
 
 def whole_weights(role_ref, rows_hbm, out_ref, counts_ref, rows_ref, sem):
@@ -192,7 +195,7 @@
                 left = k_t if f < 2 * FH else v_t
                 acc[:, f : f + WIDTH] += jnp.dot(left, steps[:tile, f : f + WIDTH], preferred_element_type=F32)
 
-        def head(slot, begin, place, blocks):
+        def head(slot, begin, blocks):
             w = weights_ref[slot]
             half = (w[:, :FH].astype(F32) * 0.5).astype(BF)
             stack[:DH] = jnp.concatenate([half, w[:, FH : 2 * FH], zero], axis=1)
@@ -205,10 +208,10 @@
                 limit = counts_ref[slot, s * UNITS + tick * (UNITS // 2)]
                 last = (start + limit - 1) // SUB
                 used = ((2 << (last - lead)) - 1) << lead
-                used = ((used | (used >> (ROWS // SUB))) >> (place // SUB)) * SUB
-                for j in range(blocks):
+                used = used | (used >> (ROWS // SUB))
+                for j, b in enumerate(blocks):
                     packed[pl.ds(pl.multiple_of(n, SUB), SUB)] = rows_ref[s, pl.ds(begin + j * SUB, SUB)]
-                    n = n + ((used >> j) & SUB)
+                    n = n + ((used >> b) & 1) * SUB
                 return n
 
             count = lax.fori_loop(0, NTOK, from_shard, jnp.int32(0))
@@ -238,11 +241,11 @@
         def both(slot, c):
             @pl.when(role == 1)
             def _():
-                head(slot, pl.multiple_of(slot * MID, SUB), jnp.where(slot == 0, EDGE, 0), MID // SUB)
+                head(slot, pl.multiple_of(slot * MID, SUB), MID_BLOCKS)
 
             @pl.when(role != 1)
             def _():
-                head(slot, 0, jnp.where(slot == 0, 0, MID), EDGE // SUB)
+                head(slot, 0, EDGE_BLOCKS)
 
             run(slot)
             return c
@@ -269,19 +272,16 @@
 def respond(tick):
     def kernel(role_ref, rows_hbm, weights_ref, *refs):
         if tick == 0:
-            prev_hbm, (out_ref, stack, down, packed, hidden, loads) = None, refs
+            prev_ref, (out_ref, stack, down, packed, hidden, loads) = None, refs
         else:
-            prev_hbm, out_ref, stack, down, packed, hidden, loads = refs
+            prev_ref, out_ref, stack, down, packed, hidden, loads = refs
         role = role_ref[0]
-        first = EDGE if tick == 0 else 0
+        first = EDGE + tick * HALF
         copies = []
         for s in range(NTOK):
             target = packed.at[pl.ds(s * HALF, HALF)]
             copies.append(pltpu.make_async_copy(rows_hbm.at[s, pl.ds(first, HALF)], target, loads.at[s]))
             copies[-1].start()
-        if tick == 1:
-            earlier = pltpu.make_async_copy(prev_hbm, out_ref.at[:, pl.ds(0, HALF)], loads.at[NTOK])
-            earlier.start()
         nothing = jnp.zeros((DH, FH), F32)
         for side in range(2):
             w = weights_ref[jnp.where(role == 2, 1, jnp.where(role == 1, side, 0))]
@@ -316,9 +316,9 @@
             gu = jnp.concatenate([w[:, :FH], w[:, FH : 2 * FH]], axis=0).T.astype(BF)
             dn = jnp.concatenate([w[:, 2 * FH :], nothing], axis=0).T.astype(BF)
             for s in range(NTOK):
+                out_ref[s, :HALF] = prev_ref[s]
                 out_ref[s, 2 * HALF : 2 * HALF + UNITS] = gu[s * UNITS : (s + 1) * UNITS]
                 out_ref[s, 2 * HALF + UNITS :] = dn[s * UNITS : (s + 1) * UNITS]
-            earlier.wait()
 
     return kernel
 
@@ -338,7 +338,7 @@
             down_ref[2 * g + h] = share[UNITS:, :DH]
 
 
-def call(kernel, outs, args, scalars=0, scratch=(), remote=(), far=False):
+def call(kernel, name, outs, args, scalars=0, scratch=(), remote=(), far=False):
     places = [pltpu.SMEM if n < scalars else pltpu.HBM if n in remote else pltpu.VMEM for n in range(len(args))]
     args = [pltpu.with_memory_space_constraint(a, p) if p == pltpu.HBM else a for a, p in zip(args, places)]
     many = isinstance(outs, (tuple, list))
@@ -347,6 +347,7 @@
         outs = pltpu.HBM(outs.shape, outs.dtype)
     return pl.pallas_call(
         kernel,
+        name=name,
         out_shape=outs,
         in_specs=[pl.BlockSpec(memory_space=p) for p in places],
         out_specs=tuple(out() for _ in outs) if many else out(),
@@ -364,7 +365,7 @@
     return result.reshape(rows.shape)
 
 
-def program(keys, values, queries, rates, counts, stagger, gate_in, up_in, down_in, entry_gate, entry_up, entry_down):
+def shards(keys, values, queries, rates, counts, stagger, gate_in, up_in, down_in, entry_gate, entry_up, entry_down):
     me = lax.axis_index("tok")
     pair = jnp.minimum(me // 3, PAIRS - 1)
     role = jnp.stack([jnp.where(me < 3 * PAIRS, me % 3, 3), pair]).astype(jnp.int32)
@@ -377,12 +378,13 @@
     scratch += [pltpu.VMEM((HEADS, UNITS, DH), BF)] * 3 + [pltpu.VMEM((NTOK, IN_ROWS, 2 * DH), BF)]
     scratch += [pltpu.SemaphoreType.DMA((6,)), pltpu.SemaphoreType.DMA((PAIRS + 1,))]
     operands = (*tokens, *shares)
-    packed0 = call(pack_first, shape(NTOK, IN_ROWS, 2 * DH), operands, 2, scratch, range(2, len(operands)), True)
+    packed0 = call(
+        pack_first, "pack_first", shape(NTOK, IN_ROWS, 2 * DH), operands, 2, scratch, range(2, len(operands)), True
+    )
     rows0 = exchange(packed0)
     tokens, queries, packed0 = lax.optimization_barrier((tokens, queries, packed0))
-    packed1 = call(pack_second, shape(NTOK, EDGE + HALF, 2 * DH), (*tokens, queries), 2)
-    packed_q = call(pack_third, shape(NTOK, HALF, 2 * DH), (queries,))
-    rows0, packed1, packed_q = lax.optimization_barrier((rows0, packed1, packed_q))
+    packed1 = call(pack_second, "pack_second", shape(NTOK, EDGE + 2 * HALF, 2 * DH), (*tokens, queries), 2)
+    rows0, packed1 = lax.optimization_barrier((rows0, packed1))
     rows1 = exchange(packed1)
     entries = jnp.concatenate(
         [lax.dynamic_slice_in_dim(e, 2 * pair, 2, 0) for e in (entry_gate, entry_up, entry_down)], axis=2
@@ -396,14 +398,21 @@
 
     def advance(tick, rows, current, limits):
         own, up, down = call(
-            gradient(tick), (weights, weight, weight), (role, limits, stagger, rows, current), 3, scratch, (3,)
+            gradient(tick),
+            "gradient",
+            (weights, weight, weight),
+            (role, limits, stagger, rows, current),
+            3,
+            scratch,
+            (3,),
         )
         below = lax.ppermute(up, "tok", UPS)
         above = lax.ppermute(down, "tok", DOWNS)
-        return call(renew, weights, (role, current, own, below, above), 1)
+        return call(renew, "renew", weights, (role, current, own, below, above), 1)
 
     current, limits = call(
         whole_weights,
+        "whole_weights",
         (weights, jax.ShapeDtypeStruct((2, FH), jnp.int32)),
         (role, rows0),
         1,
@@ -411,8 +420,6 @@
         (1,),
     )
     first = advance(0, rows0, current, limits)
-    first, packed_q = lax.optimization_barrier((first, packed_q))
-    rows_q = exchange(packed_q)
     size = lax.axis_size("block")
     passed = lax.ppermute(first, "block", [(b, b + 1) for b in range(size - 1)])
     second = advance(1, rows1, jnp.where(lax.axis_index("block") == 0, entries, passed), limits)
@@ -422,13 +429,18 @@
         pltpu.VMEM((2 * FH, 2 * DH), BF),
         pltpu.VMEM((NTOK * HALF, 2 * DH), BF),
         pltpu.VMEM((PIECE, 2 * FH), BF),
-        pltpu.SemaphoreType.DMA((NTOK + 1,)),
-    )
-    answers0 = call(respond(0), shape(NTOK, HALF, 2 * DH), (role, rows1, first), 1, scratch_q, (1,))
-    operands = (role, rows_q, second, answers0)
-    packed = call(respond(1), shape(NTOK, OUT_ROWS, 2 * DH), operands, 1, scratch_q, (1, 3))
+        pltpu.SemaphoreType.DMA((NTOK,)),
+    )
+    answers0 = call(respond(0), "respond_first", shape(NTOK, HALF, 2 * DH), (role, rows1, first), 1, scratch_q, (1,))
+    operands = (role, rows1, second, answers0)
+    packed = call(
+        respond(1), "respond_second", shape(NTOK, OUT_ROWS, 2 * DH), operands, 1, scratch_q, (1,)
+    )
     answers, gate, up, down = call(
-        unpack, (shape(2, ROWS, HEADS * DH),) + (shape(HEADS, UNITS, DH),) * 3, (exchange(packed),)
+        unpack,
+        "unpack",
+        (shape(2, ROWS, HEADS * DH),) + (shape(HEADS, UNITS, DH),) * 3,
+        (exchange(packed),),
     )
     return (answers[None], *(jnp.transpose(w, (0, 2, 1))[None] for w in (gate, up, down)))
 
@@ -437,7 +449,7 @@
     tokens = P("block", None, "tok", None)
     share = P("block", None, None, "tok")
     return jax.shard_map(
-        program,
+        shards,
         mesh=mesh,
         in_specs=(tokens,) * 5 + (P(),) + (share,) * 3 + (P(),) * 3,
         out_specs=(tokens, share, share, share),

time: 158 us -> 163 us (1.032)
  the two profiles are of different devices: /device:TPU:1 before, /device:TPU:7 now
where the time goes in v3:
time: 163 us; the launch traced here: 162 us
  Pallas kernels  46.8 us (29%)
  waiting for transfers between devices  44.2 us (27%)
  blocking collectives  32.8 us (20%)
  starting transfers between devices  30.4 us (19%)
  local copies, waits for them, and re-layouts  6.66 us (4%)
    pallas_call x10, Pallas kernels, call(): pl.pallas_call(kernel, name=name, out_shape=outs, in_specs=[pl.BlockSpec(...  46.8 us
    all_to_all x1, blocking collectives, exchange(): lax.all_to_all(rows.reshape(-1, 2 * DH), 'tok', split_axis=0, concat_axis...  32.8 us
    all_to_all x2, waiting for transfers between devices, exchange(): lax.all_to_all(rows.reshape(-1, 2 * DH), 'tok', split_axis=0, concat_axis...  20.1 us
    ppermute x2, waiting for transfers between devices, advance(): below = lax.ppermute(up, 'tok', UPS)  16.6 us
    all_to_all x2, starting transfers between devices, exchange(): lax.all_to_all(rows.reshape(-1, 2 * DH), 'tok', split_axis=0, concat_axis...  14.9 us
    ppermute x2, starting transfers between devices, advance(): below = lax.ppermute(up, 'tok', UPS)  10.4 us
    ppermute x1, waiting for transfers between devices, shards(): passed = lax.ppermute(first, 'block', [(b, b + 1) for b in range(size - 1)])  6.17 us
    unnamed x20, local copies, waits for them, and re-layouts  5.65 us
  transfers between devices with their start and end apart: 7, of which 4 were waited for; matrix products, arithmetic and copies ran while one was open for 1% of the time, Pallas kernels for 14%

profile of v3, /device:TPU:7, one launch (start us, length us, event | category | flops | bytes accessed | tf_op | source)
XLA Modules:
  0.0 162.1 jit_solution(16015331539561053455)
XLA Ops:
  2.1 3.7 %pack_first.1 = bf16[32,224,128]{2,1,0:T(8,128)(2,1)} custom-call(s32[2,20]{1,0:T(2,128)S(1)} %bitcast.35, s32[20]{0:T(128)S(1)} %copy-done.6, bf16[2,256,1280]{2,1,0:T(8,128)(2,1)} %bitcast.28, bf16[2,256,1280]{2,1,0:T(8,128)(2,1)} %bitcast.30, bf16[20,2,256]{2,1,0:T(2,128)(2,1)} %bitcast.33, bf16[20,16,64]{2,1,0:T(8,128)(2,1)} %bitcast.37, ...), custom_call_target="tpu_custom_call" | custom-call | tf_op jit(solution)/shard_map/pack_first/pallas_call | solution.py:348
  5.9 9.0 %all-to-all-start = ((bf16[32,224,128]{2,1,0:T(8,128)(2,1)}), bf16[32,224,128]{2,1,0:T(8,128)(2,1)}, u32[]{:S(2)}, u32[]{:S(2)}) async-start(bf16[32,224,128]{2,1,0:T(8,128)(2,1)} %pack_first.1), calls=%async_computation | async-start | bytes 3670016 | tf_op jit(solution)/shard_map/all_to_all | solution.py:364
  14.9 1.3 copy-done.3
  16.2 1.3 copy-done.4
  17.5 1.4 pack_second.1
  19.0 1.6 copy-done.1
  20.5 20.1 %all-to-all-done.rows_hbm = bf16[32,224,128]{2,1,0:T(8,128)(2,1)} async-done(((bf16[32,224,128]{2,1,0:T(8,128)(2,1)}), bf16[32,224,128]{2,1,0:T(8,128)(2,1)}, u32[]{:S(2)}, u32[]{:S(2)}) %all-to-all-start) | async-done | bytes 1835040 | tf_op jit(solution)/shard_map/all_to_all | solution.py:364
  40.6 6.0 %all-to-all-start.1 = ((bf16[32,352,128]{2,1,0:T(8,128)(2,1)}), bf16[32,352,128]{2,1,0:T(8,128)(2,1)}, u32[]{:S(2)}, u32[]{:S(2)}) async-start(bf16[32,352,128]{2,1,0:T(8,128)(2,1)} %copy-done.1), calls=%async_computation.1 | async-start | bytes 5767168 | tf_op jit(solution)/shard_map/all_to_all | solution.py:364
  46.7 1.8 %whole_weights.1 = (bf16[2,64,1536]{2,1,0:T(8,128)(2,1)S(1)}, s32[2,512]{1,0:T(2,128)S(1)}) custom-call(s32[2]{0:T(128)S(1)} %pad_add_fusion.role_ref, bf16[32,224,128]{2,1,0:T(8,128)(2,1)} %all-to-all-done.rows_hbm), custom_call_target="tpu_custom_call" | custom-call | tf_op jit(solution)/shard_map/whole_weights/pallas_call | solution.py:348
  48.5 10.0 %gradient.2 = (bf16[2,64,1536]{2,1,0:T(8,128)(2,1)S(1)}, bf16[64,1536]{1,0:T(8,128)(2,1)S(1)}, bf16[64,1536]{1,0:T(8,128)(2,1)S(1)}) custom-call(s32[2]{0:T(128)S(1)} %pad_add_fusion.role_ref, s32[2,512]{1,0:T(2,128)S(1)} %get-tuple-element.33.counts_ref, s32[20]{0:T(128)S(1)} %copy-done.7, bf16[32,224,128]{2,1,0:T(8,128)(2,1)} %all-to-all-done.rows_hbm, ...), custom_call_target="tpu_custom_call" | custom-call | tf_op jit(solution)/shard_map/gradient/pallas_call | solution.py:348
  58.5 3.7 %collective-permute-start = (bf16[64,1536]{1,0:T(8,128)(2,1)S(1)}, bf16[64,1536]{1,0:T(8,128)(2,1)S(1)}, u32[]{:S(2)}, u32[]{:S(2)}) collective-permute-start(bf16[64,1536]{1,0:T(8,128)(2,1)S(1)} %get-tuple-element.35), channel_id=1, source_target_pairs={{0,1},{1,2},{3,4},{4,5},{6,7},{7,8},{9,10},{10,11},{12,13},{13,14}... | collective-permute-start | bytes 589832 | tf_op jit(solution)/shard_map/ppermute | solution.py:409
  62.2 1.9 %collective-permute-start.1 = (bf16[64,1536]{1,0:T(8,128)(2,1)S(1)}, bf16[64,1536]{1,0:T(8,128)(2,1)S(1)}, u32[]{:S(2)}, u32[]{:S(2)}) collective-permute-start(bf16[64,1536]{1,0:T(8,128)(2,1)S(1)} %get-tuple-element.36), channel_id=1, source_target_pairs={{1,0},{2,1},{4,3},{5,4},{7,6},{8,7},{10,9},{11,10},{13,12},{14,13}... | collective-permute-start | bytes 589832 | tf_op jit(solution)/shard_map/ppermute | solution.py:410
  64.1 16.6 %collective-permute-done.below_ref = bf16[64,1536]{1,0:T(8,128)(2,1)S(1)} collective-permute-done((bf16[64,1536]{1,0:T(8,128)(2,1)S(1)}, bf16[64,1536]{1,0:T(8,128)(2,1)S(1)}, u32[]{:S(2)}, u32[]{:S(2)}) %collective-permute-start) | collective-permute-done | bytes 196640 | tf_op jit(solution)/shard_map/ppermute | solution.py:409
  80.8 1.4 collective-permute-done.1.above_ref
  83.1 1.3 collective-permute-start.2
  84.4 1.0 constant_dynamic-slice_fusion
  85.4 6.2 %collective-permute-done.2 = bf16[2,64,1536]{2,1,0:T(8,128)(2,1)S(1)} collective-permute-done((bf16[2,64,1536]{2,1,0:T(8,128)(2,1)S(1)}, bf16[2,64,1536]{2,1,0:T(8,128)(2,1)S(1)}, u32[]{:S(2)}, u32[]{:S(2)}) %collective-permute-start.2) | collective-permute-done | bytes 393248 | tf_op jit(solution)/shard_map/ppermute | solution.py:424
  91.7 10.1 %gradient.3 = (bf16[2,64,1536]{2,1,0:T(8,128)(2,1)S(1)}, bf16[64,1536]{1,0:T(8,128)(2,1)S(1)}, bf16[64,1536]{1,0:T(8,128)(2,1)S(1)}) custom-call(s32[2]{0:T(128)S(1)} %pad_add_fusion.role_ref, s32[2,512]{1,0:T(2,128)S(1)} %get-tuple-element.33.counts_ref, s32[20]{0:T(128)S(1)} %copy-done.7, bf16[32,352,128]{2,1,0:T(8,128)(2,1)} %all-to-all-done.1.rows_hbm, ...), custom_call_target="tpu_custom_call" | custom-call | tf_op jit(solution)/shard_map/gradient/pallas_call | solution.py:348
  101.8 6.7 %collective-permute-start.3 = (bf16[64,1536]{1,0:T(8,128)(2,1)S(1)}, bf16[64,1536]{1,0:T(8,128)(2,1)S(1)}, u32[]{:S(2)}, u32[]{:S(2)}) collective-permute-start(bf16[64,1536]{1,0:T(8,128)(2,1)S(1)} %get-tuple-element.38), channel_id=1, source_target_pairs={{0,1},{1,2},{3,4},{4,5},{6,7},{7,8},{9,10},{10,11},{12,13},{13,14}... | collective-permute-start | bytes 589832 | tf_op jit(solution)/shard_map/ppermute | solution.py:409
  108.5 1.9 %collective-permute-start.4 = (bf16[64,1536]{1,0:T(8,128)(2,1)S(1)}, bf16[64,1536]{1,0:T(8,128)(2,1)S(1)}, u32[]{:S(2)}, u32[]{:S(2)}) collective-permute-start(bf16[64,1536]{1,0:T(8,128)(2,1)S(1)} %get-tuple-element.39), channel_id=1, source_target_pairs={{1,0},{2,1},{4,3},{5,4},{7,6},{8,7},{10,9},{11,10},{13,12},{14,13}... | collective-permute-start | bytes 589832 | tf_op jit(solution)/shard_map/ppermute | solution.py:410
  110.4 8.1 %respond_first.1.refs_0_ = bf16[32,88,128]{2,1,0:T(8,128)(2,1)S(1)} custom-call(s32[2]{0:T(128)S(1)} %pad_add_fusion.role_ref, bf16[32,352,128]{2,1,0:T(8,128)(2,1)} %all-to-all-done.1.rows_hbm, bf16[2,64,1536]{2,1,0:T(8,128)(2,1)S(1)} %renew.2.weights_ref), custom_call_target="tpu_custom_call" | custom-call | tf_op jit(solution)/shard_map/respond_first/pallas_call | solution.py:348
  119.6 8.3 %respond_second.1 = bf16[32,208,128]{2,1,0:T(8,128)(2,1)S(1)} custom-call(s32[2]{0:T(128)S(1)} %pad_add_fusion.role_ref, bf16[32,352,128]{2,1,0:T(8,128)(2,1)} %all-to-all-done.1.rows_hbm, bf16[2,64,1536]{2,1,0:T(8,128)(2,1)S(1)} %renew.3.weights_ref, bf16[32,88,128]{2,1,0:T(8,128)(2,1)S(1)} %respond_first.1.refs_0_), custom_call_target="tpu_custom_call" | custom-call | tf_op jit(solution)/shard_map/respond_second/pallas_call | solution.py:348
  127.8 32.8 %all_to_all.18.rows_ref = bf16[32,208,128]{2,1,0:T(8,128)(2,1)S(1)} all-to-all(bf16[32,208,128]{2,1,0:T(8,128)(2,1)S(1)} %respond_second.1), channel_id=1, replica_groups=mesh['block'=4,'tok'=32] {'tok'}, dimensions={0} | all-to-all | bytes 3407872 | tf_op jit(solution)/shard_map/all_to_all | solution.py:364
  160.6 1.5 unpack.1
  (25 shorter events, 3.6 us)
Async XLA Ops:
  0.6 83.8 %copy-start = (bf16[20,64,512]{2,1,0:T(8,128)(2,1)S(1)}, bf16[20,64,512]{2,1,0:T(8,128)(2,1)}, u32[]{:S(2)}) copy-start(bf16[20,64,512]{2,1,0:T(8,128)(2,1)} %param.21) | copy-start | bytes 3932164
  0.6 0.8 copy-start.6
  1.4 0.7 copy-start.8
  5.8 9.0 %copy-start.2 = (bf16[1,2,256,1280]{3,2,1,0:T(8,128)(2,1)S(1)}, bf16[1,2,256,1280]{3,2,1,0:T(8,128)(2,1)}, u32[]{:S(2)}) copy-start(bf16[1,2,256,1280]{3,2,1,0:T(8,128)(2,1)} %param.12) | copy-start | bytes 3932164
  5.8 9.0 %copy-start.5 = (bf16[1,2,256,20]{2,1,3,0:T(2,128)(2,1)S(1)}, bf16[1,2,256,20]{2,1,3,0:T(2,128)(2,1)}, u32[]{:S(2)}) copy-start(bf16[1,2,256,20]{2,1,3,0:T(2,128)(2,1)} %param.15) | copy-start | bytes 61444
  5.9 9.0 %copy-start.7 = (s32[20]{0:T(128)S(1)}, s32[20]{0:T(128)}, u32[]{:S(2)}) copy-start(s32[20]{0:T(128)} %stagger_ref.6) | copy-start | bytes 244
  5.9 9.0 %copy-start.9 = (s32[1,2,1,20]{3,2,1,0:T(1,128)S(1)}, s32[1,2,1,20]{3,2,1,0:T(1,128)}, u32[]{:S(2)}) copy-start(s32[1,2,1,20]{3,2,1,0:T(1,128)} %param.16) | copy-start | bytes 484
  5.9 34.7 %all-to-all-start = ((bf16[32,224,128]{2,1,0:T(8,128)(2,1)}), bf16[32,224,128]{2,1,0:T(8,128)(2,1)}, u32[]{:S(2)}, u32[]{:S(2)}) async-start(bf16[32,224,128]{2,1,0:T(8,128)(2,1)} %pack_first.1), calls=%async_computation | async-start | bytes 3670016 | tf_op jit(solution)/shard_map/all_to_all | solution.py:364
  14.9 1.3 copy-start.3
  16.2 1.3 copy-start.4
  19.0 1.6 copy-start.1
  40.6 51.1 %all-to-all-start.1 = ((bf16[32,352,128]{2,1,0:T(8,128)(2,1)}), bf16[32,352,128]{2,1,0:T(8,128)(2,1)}, u32[]{:S(2)}, u32[]{:S(2)}) async-start(bf16[32,352,128]{2,1,0:T(8,128)(2,1)} %copy-done.1), calls=%async_computation.1 | async-start | bytes 5767168 | tf_op jit(solution)/shard_map/all_to_all | solution.py:364
  58.5 22.3 %collective-permute-start = (bf16[64,1536]{1,0:T(8,128)(2,1)S(1)}, bf16[64,1536]{1,0:T(8,128)(2,1)S(1)}, u32[]{:S(2)}, u32[]{:S(2)}) collective-permute-start(bf16[64,1536]{1,0:T(8,128)(2,1)S(1)} %get-tuple-element.35), channel_id=1, source_target_pairs={{0,1},{1,2},{3,4},{4,5},{6,7},{7,8},{9,10},{10,11},{12,13},{13,14}... | collective-permute-start | bytes 589832 | tf_op jit(solution)/shard_map/ppermute | solution.py:409
  62.2 19.9 %collective-permute-start.1 = (bf16[64,1536]{1,0:T(8,128)(2,1)S(1)}, bf16[64,1536]{1,0:T(8,128)(2,1)S(1)}, u32[]{:S(2)}, u32[]{:S(2)}) collective-permute-start(bf16[64,1536]{1,0:T(8,128)(2,1)S(1)} %get-tuple-element.36), channel_id=1, source_target_pairs={{1,0},{2,1},{4,3},{5,4},{7,6},{8,7},{10,9},{11,10},{13,12},{14,13}... | collective-permute-start | bytes 589832 | tf_op jit(solution)/shard_map/ppermute | solution.py:410
  83.1 8.5 %collective-permute-start.2 = (bf16[2,64,1536]{2,1,0:T(8,128)(2,1)S(1)}, bf16[2,64,1536]{2,1,0:T(8,128)(2,1)S(1)}, u32[]{:S(2)}, u32[]{:S(2)}) collective-permute-start(bf16[2,64,1536]{2,1,0:T(8,128)(2,1)S(1)} %renew.2.weights_ref), channel_id=1, source_target_pairs={{0,32},{32,64},{64,96},{1,33},{33,65},{65,97},{2,34},{34,66},{66,9... | collective-permute-start | bytes 1179656 | tf_op jit(solution)/shard_map/ppermute | solution.py:424
  101.8 16.8 %collective-permute-start.3 = (bf16[64,1536]{1,0:T(8,128)(2,1)S(1)}, bf16[64,1536]{1,0:T(8,128)(2,1)S(1)}, u32[]{:S(2)}, u32[]{:S(2)}) collective-permute-start(bf16[64,1536]{1,0:T(8,128)(2,1)S(1)} %get-tuple-element.38), channel_id=1, source_target_pairs={{0,1},{1,2},{3,4},{4,5},{6,7},{7,8},{9,10},{10,11},{12,13},{13,14}... | collective-permute-start | bytes 589832 | tf_op jit(solution)/shard_map/ppermute | solution.py:409
  108.5 10.1 %collective-permute-start.4 = (bf16[64,1536]{1,0:T(8,128)(2,1)S(1)}, bf16[64,1536]{1,0:T(8,128)(2,1)S(1)}, u32[]{:S(2)}, u32[]{:S(2)}) collective-permute-start(bf16[64,1536]{1,0:T(8,128)(2,1)S(1)} %get-tuple-element.39), channel_id=1, source_target_pairs={{1,0},{2,1},{4,3},{5,4},{7,6},{8,7},{10,9},{11,10},{13,12},{14,13}... | collective-permute-start | bytes 589832 | tf_op jit(solution)/shard_map/ppermute | solution.py:410

commit v4 on v2

--- a/solution.py
+++ b/solution.py
@@ -23,6 +23,8 @@
 TILE = 512
 SHARE = 2 * UNITS
 IN_ROWS = 224
+MID_BLOCKS = (1, 4, 7, 10, 13)
+EDGE_BLOCKS = tuple(b for b in range(ROWS // SUB) if b not in MID_BLOCKS)
 HALF = EDGE // 2
 OUT_ROWS = 2 * HALF + SHARE
 WIDTH = 256
@@ -46,10 +48,14 @@
 
 
 def scatter_rows(out_ref, g, first, second):
-    out_ref[3 * g, 0:EDGE] = first[0:EDGE]
-    out_ref[3 * g + 1, 0:MID] = first[EDGE:ROWS]
-    out_ref[3 * g + 1, MID : 2 * MID] = second[0:MID]
-    out_ref[3 * g + 2, 0:EDGE] = second[MID:ROWS]
+    for j, b in enumerate(EDGE_BLOCKS):
+        to, of = slice(j * SUB, (j + 1) * SUB), slice(b * SUB, (b + 1) * SUB)
+        out_ref[3 * g, to] = first[of]
+        out_ref[3 * g + 2, to] = second[of]
+    for j, b in enumerate(MID_BLOCKS):
+        of = slice(b * SUB, (b + 1) * SUB)
+        out_ref[3 * g + 1, j * SUB : (j + 1) * SUB] = first[of]
+        out_ref[3 * g + 1, MID + j * SUB : MID + (j + 1) * SUB] = second[of]
 
 
 def spread_of():
@@ -192,7 +198,7 @@
                 left = k_t if f < 2 * FH else v_t
                 acc[:, f : f + WIDTH] += jnp.dot(left, steps[:tile, f : f + WIDTH], preferred_element_type=F32)
 
-        def head(slot, begin, place, blocks):
+        def head(slot, begin, blocks):
             w = weights_ref[slot]
             half = (w[:, :FH].astype(F32) * 0.5).astype(BF)
             stack[:DH] = jnp.concatenate([half, w[:, FH : 2 * FH], zero], axis=1)
@@ -205,10 +211,10 @@
                 limit = counts_ref[slot, s * UNITS + tick * (UNITS // 2)]
                 last = (start + limit - 1) // SUB
                 used = ((2 << (last - lead)) - 1) << lead
-                used = ((used | (used >> (ROWS // SUB))) >> (place // SUB)) * SUB
-                for j in range(blocks):
+                used = used | (used >> (ROWS // SUB))
+                for j, b in enumerate(blocks):
                     packed[pl.ds(pl.multiple_of(n, SUB), SUB)] = rows_ref[s, pl.ds(begin + j * SUB, SUB)]
-                    n = n + ((used >> j) & SUB)
+                    n = n + ((used >> b) & 1) * SUB
                 return n
 
             count = lax.fori_loop(0, NTOK, from_shard, jnp.int32(0))
@@ -238,11 +244,11 @@
         def both(slot, c):
             @pl.when(role == 1)
             def _():
-                head(slot, pl.multiple_of(slot * MID, SUB), jnp.where(slot == 0, EDGE, 0), MID // SUB)
+                head(slot, pl.multiple_of(slot * MID, SUB), MID_BLOCKS)
 
             @pl.when(role != 1)
             def _():
-                head(slot, 0, jnp.where(slot == 0, 0, MID), EDGE // SUB)
+                head(slot, 0, EDGE_BLOCKS)
 
             run(slot)
             return c
@@ -267,21 +273,20 @@
 
 
 def respond(tick):
-    def kernel(role_ref, rows_hbm, weights_ref, *refs):
+    def kernel(role_ref, rows_ref, weights_ref, *refs):
         if tick == 0:
-            prev_hbm, (out_ref, stack, down, packed, hidden, loads) = None, refs
+            prev_ref, (out_ref, stack, down, packed, hidden, loads) = None, refs
         else:
-            prev_hbm, out_ref, stack, down, packed, hidden, loads = refs
+            prev_ref, out_ref, stack, down, packed, hidden, loads = refs
         role = role_ref[0]
-        first = EDGE if tick == 0 else 0
         copies = []
         for s in range(NTOK):
+            if tick == 1:
+                packed[s * HALF : (s + 1) * HALF] = rows_ref[s]
+                continue
             target = packed.at[pl.ds(s * HALF, HALF)]
-            copies.append(pltpu.make_async_copy(rows_hbm.at[s, pl.ds(first, HALF)], target, loads.at[s]))
+            copies.append(pltpu.make_async_copy(rows_ref.at[s, pl.ds(EDGE, HALF)], target, loads.at[s]))
             copies[-1].start()
-        if tick == 1:
-            earlier = pltpu.make_async_copy(prev_hbm, out_ref.at[:, pl.ds(0, HALF)], loads.at[NTOK])
-            earlier.start()
         nothing = jnp.zeros((DH, FH), F32)
         for side in range(2):
             w = weights_ref[jnp.where(role == 2, 1, jnp.where(role == 1, side, 0))]
@@ -316,9 +321,9 @@
             gu = jnp.concatenate([w[:, :FH], w[:, FH : 2 * FH]], axis=0).T.astype(BF)
             dn = jnp.concatenate([w[:, 2 * FH :], nothing], axis=0).T.astype(BF)
             for s in range(NTOK):
+                out_ref[s, :HALF] = prev_ref[s]
                 out_ref[s, 2 * HALF : 2 * HALF + UNITS] = gu[s * UNITS : (s + 1) * UNITS]
                 out_ref[s, 2 * HALF + UNITS :] = dn[s * UNITS : (s + 1) * UNITS]
-            earlier.wait()
 
     return kernel
 
@@ -422,11 +427,11 @@
         pltpu.VMEM((2 * FH, 2 * DH), BF),
         pltpu.VMEM((NTOK * HALF, 2 * DH), BF),
         pltpu.VMEM((PIECE, 2 * FH), BF),
-        pltpu.SemaphoreType.DMA((NTOK + 1,)),
+        pltpu.SemaphoreType.DMA((NTOK,)),
     )
     answers0 = call(respond(0), shape(NTOK, HALF, 2 * DH), (role, rows1, first), 1, scratch_q, (1,))
     operands = (role, rows_q, second, answers0)
-    packed = call(respond(1), shape(NTOK, OUT_ROWS, 2 * DH), operands, 1, scratch_q, (1, 3))
+    packed = call(respond(1), shape(NTOK, OUT_ROWS, 2 * DH), operands, 1, scratch_q)
     answers, gate, up, down = call(
         unpack, (shape(2, ROWS, HEADS * DH),) + (shape(HEADS, UNITS, DH),) * 3, (exchange(packed),)
     )

time: 158 us -> 154 us (0.975)
  the two profiles are of different devices: /device:TPU:1 before, /device:TPU:7 now
where the time goes in v4:
time: 154 us; the launch traced here: 153 us
  Pallas kernels  50 us (32%)
  starting transfers between devices  34.3 us (22%)
  blocking collectives  32.2 us (21%)
  waiting for transfers between devices  31.3 us (20%)
  local copies, waits for them, and re-layouts  3.89 us (3%)
    pallas_call x11, Pallas kernels, call(): pl.pallas_call(kernel, out_shape=outs, in_specs=[pl.BlockSpec(memory_spac...  50 us
    all_to_all x1, blocking collectives, exchange(): lax.all_to_all(rows.reshape(-1, 2 * DH), 'tok', split_axis=0, concat_axis...  32.2 us
    all_to_all x3, starting transfers between devices, exchange(): lax.all_to_all(rows.reshape(-1, 2 * DH), 'tok', split_axis=0, concat_axis...  21.8 us
    all_to_all x3, waiting for transfers between devices, exchange(): lax.all_to_all(rows.reshape(-1, 2 * DH), 'tok', split_axis=0, concat_axis...  20.6 us
    ppermute x2, waiting for transfers between devices, advance(): below = lax.ppermute(up, 'tok', UPS)  8.35 us
    ppermute x2, starting transfers between devices, advance(): below = lax.ppermute(up, 'tok', UPS)  7.3 us
    ppermute x2, starting transfers between devices, advance(): above = lax.ppermute(down, 'tok', DOWNS)  3.84 us
  transfers between devices with their start and end apart: 8, of which 3 were waited for; matrix products, arithmetic and copies ran while one was open for 1% of the time, Pallas kernels for 24%

profile of v4, /device:TPU:7, one launch (start us, length us, event | category | flops | bytes accessed | tf_op | source)
XLA Modules:
  0.0 152.8 jit_solution(9417663290124597899)
XLA Ops:
  2.1 3.7 %shard_map.147 = bf16[32,224,128]{2,1,0:T(8,128)(2,1)} custom-call(s32[2,20]{1,0:T(2,128)S(1)} %bitcast.36, s32[20]{0:T(128)S(1)} %copy-done.5, bf16[2,256,1280]{2,1,0:T(8,128)(2,1)} %bitcast.28, bf16[2,256,1280]{2,1,0:T(8,128)(2,1)} %bitcast.30, bf16[20,2,256]{2,1,0:T(2,128)(2,1)} %bitcast.34, bf16[20,16,64]{2,1,0:T(8,128)(2,1)} %bitcast.38, ...), custom_call_target="tpu_custom_call" | custom-call | tf_op jit(solution)/shard_map/pallas_call | solution.py:353
  5.8 9.0 %all-to-all-start = ((bf16[32,224,128]{2,1,0:T(8,128)(2,1)}), bf16[32,224,128]{2,1,0:T(8,128)(2,1)}, u32[]{:S(2)}, u32[]{:S(2)}) async-start(bf16[32,224,128]{2,1,0:T(8,128)(2,1)} %shard_map.147), calls=%async_computation | async-start | bytes 3670016 | tf_op jit(solution)/shard_map/all_to_all | solution.py:368
  14.8 1.4 copy-done.3
  16.2 1.0 shard_map.149
  17.3 2.7 %shard_map.148 = bf16[32,264,128]{2,1,0:T(8,128)(2,1)} custom-call(s32[2,20]{1,0:T(2,128)S(1)} %bitcast.37, s32[20]{0:T(128)S(1)} %copy-done.6, bf16[2,256,1280]{2,1,0:T(8,128)(2,1)S(1)} %bitcast.29, bf16[2,256,1280]{2,1,0:T(8,128)(2,1)S(1)} %bitcast.31, bf16[20,2,256]{2,1,0:T(2,128)(2,1)S(1)} %bitcast.35, bf16[2,256,1280]{2,1,0:T(8,128)(2,1)S(1)} %bitcast.33), custom_call_target="tpu_custom_call" | custom-call | tf_op jit(solution)/shard_map/pallas_call | solution.py:353
  20.0 20.6 %all-to-all-done.rows_hbm = bf16[32,224,128]{2,1,0:T(8,128)(2,1)} async-done(((bf16[32,224,128]{2,1,0:T(8,128)(2,1)}), bf16[32,224,128]{2,1,0:T(8,128)(2,1)}, u32[]{:S(2)}, u32[]{:S(2)}) %all-to-all-start) | async-done | bytes 1835040 | tf_op jit(solution)/shard_map/all_to_all | solution.py:368
  40.6 5.9 %all-to-all-start.2 = ((bf16[32,264,128]{2,1,0:T(8,128)(2,1)}), bf16[32,264,128]{2,1,0:T(8,128)(2,1)}, u32[]{:S(2)}, u32[]{:S(2)}) async-start(bf16[32,264,128]{2,1,0:T(8,128)(2,1)} %shard_map.148), calls=%async_computation.2 | async-start | bytes 4325376 | tf_op jit(solution)/shard_map/all_to_all | solution.py:368
  46.6 1.8 %shard_map.150 = (bf16[2,64,1536]{2,1,0:T(8,128)(2,1)S(1)}, s32[2,512]{1,0:T(2,128)S(1)}) custom-call(s32[2]{0:T(128)S(1)} %pad_add_fusion.role_ref, bf16[32,224,128]{2,1,0:T(8,128)(2,1)} %all-to-all-done.rows_hbm), custom_call_target="tpu_custom_call" | custom-call | tf_op jit(solution)/shard_map/pallas_call | solution.py:353
  48.4 10.6 %shard_map.151 = (bf16[2,64,1536]{2,1,0:T(8,128)(2,1)S(1)}, bf16[64,1536]{1,0:T(8,128)(2,1)S(1)}, bf16[64,1536]{1,0:T(8,128)(2,1)S(1)}) custom-call(s32[2]{0:T(128)S(1)} %pad_add_fusion.role_ref, s32[2,512]{1,0:T(2,128)S(1)} %get-tuple-element.35.counts_ref, s32[20]{0:T(128)S(1)} %copy-done.6, bf16[32,224,128]{2,1,0:T(8,128)(2,1)} %all-to-all-done.rows_hbm, ...), custom_call_target="tpu_custom_call" | custom-call | tf_op jit(solution)/shard_map/pallas_call | solution.py:353
  59.0 3.1 %collective-permute-start = (bf16[64,1536]{1,0:T(8,128)(2,1)S(1)}, bf16[64,1536]{1,0:T(8,128)(2,1)S(1)}, u32[]{:S(2)}, u32[]{:S(2)}) collective-permute-start(bf16[64,1536]{1,0:T(8,128)(2,1)S(1)} %get-tuple-element.37), channel_id=1, source_target_pairs={{0,1},{1,2},{3,4},{4,5},{6,7},{7,8},{9,10},{10,11},{12,13},{13,14}... | collective-permute-start | bytes 589832 | tf_op jit(solution)/shard_map/ppermute | solution.py:406
  62.1 1.9 %collective-permute-start.1 = (bf16[64,1536]{1,0:T(8,128)(2,1)S(1)}, bf16[64,1536]{1,0:T(8,128)(2,1)S(1)}, u32[]{:S(2)}, u32[]{:S(2)}) collective-permute-start(bf16[64,1536]{1,0:T(8,128)(2,1)S(1)} %get-tuple-element.38), channel_id=1, source_target_pairs={{1,0},{2,1},{4,3},{5,4},{7,6},{8,7},{10,9},{11,10},{13,12},{14,13}... | collective-permute-start | bytes 589832 | tf_op jit(solution)/shard_map/ppermute | solution.py:407
  64.1 8.3 %collective-permute-done.below_ref = bf16[64,1536]{1,0:T(8,128)(2,1)S(1)} collective-permute-done((bf16[64,1536]{1,0:T(8,128)(2,1)S(1)}, bf16[64,1536]{1,0:T(8,128)(2,1)S(1)}, u32[]{:S(2)}, u32[]{:S(2)}) %collective-permute-start) | collective-permute-done | bytes 196640 | tf_op jit(solution)/shard_map/ppermute | solution.py:406
  72.4 2.4 %collective-permute-done.1.above_ref = bf16[64,1536]{1,0:T(8,128)(2,1)S(1)} collective-permute-done((bf16[64,1536]{1,0:T(8,128)(2,1)S(1)}, bf16[64,1536]{1,0:T(8,128)(2,1)S(1)}, u32[]{:S(2)}, u32[]{:S(2)}) %collective-permute-start.1) | collective-permute-done | bytes 196640 | tf_op jit(solution)/shard_map/ppermute | solution.py:407
  75.7 1.3 collective-permute-start.2
  77.1 1.0 constant_dynamic-slice_fusion
  78.1 6.9 %all-to-all-start.1 = ((bf16[32,88,128]{2,1,0:T(8,128)(2,1)}), bf16[32,88,128]{2,1,0:T(8,128)(2,1)S(1)}, u32[]{:S(2)}, u32[]{:S(2)}) async-start(bf16[32,88,128]{2,1,0:T(8,128)(2,1)} %shard_map.149), calls=%async_computation.1 | async-start | bytes 1441792 | tf_op jit(solution)/shard_map/all_to_all | solution.py:368
  85.2 11.3 %shard_map.153 = (bf16[2,64,1536]{2,1,0:T(8,128)(2,1)S(1)}, bf16[64,1536]{1,0:T(8,128)(2,1)S(1)}, bf16[64,1536]{1,0:T(8,128)(2,1)S(1)}) custom-call(s32[2]{0:T(128)S(1)} %pad_add_fusion.role_ref, s32[2,512]{1,0:T(2,128)S(1)} %get-tuple-element.35.counts_ref, s32[20]{0:T(128)S(1)} %copy-done.6, bf16[32,264,128]{2,1,0:T(8,128)(2,1)} %all-to-all-done.2.rows_hbm.rows_ref, ...), custom_call_target="tpu_custom_call" | custom-call | tf_op jit(solution)/shard_map/pallas_call | solution.py:353
  96.4 4.2 %collective-permute-start.3 = (bf16[64,1536]{1,0:T(8,128)(2,1)S(1)}, bf16[64,1536]{1,0:T(8,128)(2,1)S(1)}, u32[]{:S(2)}, u32[]{:S(2)}) collective-permute-start(bf16[64,1536]{1,0:T(8,128)(2,1)S(1)} %get-tuple-element.44), channel_id=1, source_target_pairs={{0,1},{1,2},{3,4},{4,5},{6,7},{7,8},{9,10},{10,11},{12,13},{13,14}... | collective-permute-start | bytes 589832 | tf_op jit(solution)/shard_map/ppermute | solution.py:406
  100.6 1.9 %collective-permute-start.4 = (bf16[64,1536]{1,0:T(8,128)(2,1)S(1)}, bf16[64,1536]{1,0:T(8,128)(2,1)S(1)}, u32[]{:S(2)}, u32[]{:S(2)}) collective-permute-start(bf16[64,1536]{1,0:T(8,128)(2,1)S(1)} %get-tuple-element.45), channel_id=1, source_target_pairs={{1,0},{2,1},{4,3},{5,4},{7,6},{8,7},{10,9},{11,10},{13,12},{14,13}... | collective-permute-start | bytes 589832 | tf_op jit(solution)/shard_map/ppermute | solution.py:407
  102.6 8.1 %shard_map.155.refs_0_ = bf16[32,88,128]{2,1,0:T(8,128)(2,1)S(1)} custom-call(s32[2]{0:T(128)S(1)} %pad_add_fusion.role_ref, bf16[32,264,128]{2,1,0:T(8,128)(2,1)} %all-to-all-done.2.rows_hbm.rows_ref, bf16[2,64,1536]{2,1,0:T(8,128)(2,1)S(1)} %shard_map.152.weights_ref), custom_call_target="tpu_custom_call" | custom-call | tf_op jit(solution)/shard_map/pallas_call | solution.py:353
  110.7 0.9 shard_map.154.weights_ref
  111.7 7.4 %shard_map.156 = bf16[32,208,128]{2,1,0:T(8,128)(2,1)S(1)} custom-call(s32[2]{0:T(128)S(1)} %pad_add_fusion.role_ref, bf16[32,88,128]{2,1,0:T(8,128)(2,1)S(1)} %all-to-all-done.1.rows_ref, bf16[2,64,1536]{2,1,0:T(8,128)(2,1)S(1)} %shard_map.154.weights_ref, bf16[32,88,128]{2,1,0:T(8,128)(2,1)S(1)} %shard_map.155.refs_0_), custom_call_target="tpu_custom_call" | custom-call | tf_op jit(solution)/shard_map/pallas_call | solution.py:353
  119.1 32.2 %all_to_all.24.rows_ref = bf16[32,208,128]{2,1,0:T(8,128)(2,1)S(1)} all-to-all(bf16[32,208,128]{2,1,0:T(8,128)(2,1)S(1)} %shard_map.156), channel_id=1, replica_groups=mesh['block'=4,'tok'=32] {'tok'}, dimensions={0} | all-to-all | bytes 3407872 | tf_op jit(solution)/shard_map/all_to_all | solution.py:368
  151.3 1.5 shard_map.157
  (26 shorter events, 2.6 us)
Async XLA Ops:
  0.6 84.4 %copy-start = (bf16[20,64,512]{2,1,0:T(8,128)(2,1)S(1)}, bf16[20,64,512]{2,1,0:T(8,128)(2,1)}, u32[]{:S(2)}) copy-start(bf16[20,64,512]{2,1,0:T(8,128)(2,1)} %param.21) | copy-start | bytes 3932164
  0.6 0.8 copy-start.5
  1.4 0.7 copy-start.7
  5.8 11.5 %copy-start.2 = (bf16[1,2,256,1280]{3,2,1,0:T(8,128)(2,1)S(1)}, bf16[1,2,256,1280]{3,2,1,0:T(8,128)(2,1)}, u32[]{:S(2)}) copy-start(bf16[1,2,256,1280]{3,2,1,0:T(8,128)(2,1)} %param.13) | copy-start | bytes 3932164
  5.8 34.7 %all-to-all-start = ((bf16[32,224,128]{2,1,0:T(8,128)(2,1)}), bf16[32,224,128]{2,1,0:T(8,128)(2,1)}, u32[]{:S(2)}, u32[]{:S(2)}) async-start(bf16[32,224,128]{2,1,0:T(8,128)(2,1)} %shard_map.147), calls=%async_computation | async-start | bytes 3670016 | tf_op jit(solution)/shard_map/all_to_all | solution.py:368
  14.8 2.5 %copy-start.1 = (bf16[1,2,256,1280]{3,2,1,0:T(8,128)(2,1)S(1)}, bf16[1,2,256,1280]{3,2,1,0:T(8,128)(2,1)}, u32[]{:S(2)}) copy-start(bf16[1,2,256,1280]{3,2,1,0:T(8,128)(2,1)} %param.12) | copy-start | bytes 3932164
  14.8 1.4 copy-start.3
  16.2 1.0 copy-start.4
  16.2 1.0 copy-start.6
  16.2 1.1 copy-start.8
  40.6 37.5 %all-to-all-start.2 = ((bf16[32,264,128]{2,1,0:T(8,128)(2,1)}), bf16[32,264,128]{2,1,0:T(8,128)(2,1)}, u32[]{:S(2)}, u32[]{:S(2)}) async-start(bf16[32,264,128]{2,1,0:T(8,128)(2,1)} %shard_map.148), calls=%async_computation.2 | async-start | bytes 4325376 | tf_op jit(solution)/shard_map/all_to_all | solution.py:368
  59.0 13.4 %collective-permute-start = (bf16[64,1536]{1,0:T(8,128)(2,1)S(1)}, bf16[64,1536]{1,0:T(8,128)(2,1)S(1)}, u32[]{:S(2)}, u32[]{:S(2)}) collective-permute-start(bf16[64,1536]{1,0:T(8,128)(2,1)S(1)} %get-tuple-element.37), channel_id=1, source_target_pairs={{0,1},{1,2},{3,4},{4,5},{6,7},{7,8},{9,10},{10,11},{12,13},{13,14}... | collective-permute-start | bytes 589832 | tf_op jit(solution)/shard_map/ppermute | solution.py:406
  62.1 12.6 %collective-permute-start.1 = (bf16[64,1536]{1,0:T(8,128)(2,1)S(1)}, bf16[64,1536]{1,0:T(8,128)(2,1)S(1)}, u32[]{:S(2)}, u32[]{:S(2)}) collective-permute-start(bf16[64,1536]{1,0:T(8,128)(2,1)S(1)} %get-tuple-element.38), channel_id=1, source_target_pairs={{1,0},{2,1},{4,3},{5,4},{7,6},{8,7},{10,9},{11,10},{13,12},{14,13}... | collective-permute-start | bytes 589832 | tf_op jit(solution)/shard_map/ppermute | solution.py:407
  75.7 9.3 %collective-permute-start.2 = (bf16[2,64,1536]{2,1,0:T(8,128)(2,1)S(1)}, bf16[2,64,1536]{2,1,0:T(8,128)(2,1)S(1)}, u32[]{:S(2)}, u32[]{:S(2)}) collective-permute-start(bf16[2,64,1536]{2,1,0:T(8,128)(2,1)S(1)} %shard_map.152.weights_ref), channel_id=1, source_target_pairs={{0,32},{32,64},{64,96},{1,33},{33,65},{65,97},{2,34},{34,66},{66,9... | collective-permute-start | bytes 1179656 | tf_op jit(solution)/shard_map/ppermute | solution.py:422
  78.1 33.6 %all-to-all-start.1 = ((bf16[32,88,128]{2,1,0:T(8,128)(2,1)}), bf16[32,88,128]{2,1,0:T(8,128)(2,1)S(1)}, u32[]{:S(2)}, u32[]{:S(2)}) async-start(bf16[32,88,128]{2,1,0:T(8,128)(2,1)} %shard_map.149), calls=%async_computation.1 | async-start | bytes 1441792 | tf_op jit(solution)/shard_map/all_to_all | solution.py:368
  96.4 14.3 %collective-permute-start.3 = (bf16[64,1536]{1,0:T(8,128)(2,1)S(1)}, bf16[64,1536]{1,0:T(8,128)(2,1)S(1)}, u32[]{:S(2)}, u32[]{:S(2)}) collective-permute-start(bf16[64,1536]{1,0:T(8,128)(2,1)S(1)} %get-tuple-element.44), channel_id=1, source_target_pairs={{0,1},{1,2},{3,4},{4,5},{6,7},{7,8},{9,10},{10,11},{12,13},{13,14}... | collective-permute-start | bytes 589832 | tf_op jit(solution)/shard_map/ppermute | solution.py:406
  100.6 10.1 %collective-permute-start.4 = (bf16[64,1536]{1,0:T(8,128)(2,1)S(1)}, bf16[64,1536]{1,0:T(8,128)(2,1)S(1)}, u32[]{:S(2)}, u32[]{:S(2)}) collective-permute-start(bf16[64,1536]{1,0:T(8,128)(2,1)S(1)} %get-tuple-element.45), channel_id=1, source_target_pairs={{1,0},{2,1},{4,3},{5,4},{7,6},{8,7},{10,9},{11,10},{13,12},{14,13}... | collective-permute-start | bytes 589832 | tf_op jit(solution)/shard_map/ppermute | solution.py:407

commit v5 on v4

--- a/solution.py
+++ b/solution.py
@@ -399,10 +399,14 @@
     scratch = (*stacked, pltpu.VMEM((PACKED, 2 * DH), BF), pltpu.VMEM((TILE, 3 * FH), BF), pltpu.SMEM((1,), jnp.int32))
     scratch += (pltpu.VMEM((NTOK, EDGE, 2 * DH), BF), pltpu.SemaphoreType.DMA)
 
+    waiting = [packed_q]
+
     def advance(tick, rows, current, limits):
         own, up, down = call(
             gradient(tick), (weights, weight, weight), (role, limits, stagger, rows, current), 3, scratch, (3,)
         )
+        if tick == 1:
+            own, waiting[0] = lax.optimization_barrier((own, waiting[0]))
         below = lax.ppermute(up, "tok", UPS)
         above = lax.ppermute(down, "tok", DOWNS)
         return call(renew, weights, (role, current, own, below, above), 1)
@@ -416,12 +420,11 @@
         (1,),
     )
     first = advance(0, rows0, current, limits)
-    first, packed_q = lax.optimization_barrier((first, packed_q))
-    rows_q = exchange(packed_q)
     size = lax.axis_size("block")
     passed = lax.ppermute(first, "block", [(b, b + 1) for b in range(size - 1)])
     second = advance(1, rows1, jnp.where(lax.axis_index("block") == 0, entries, passed), limits)
 
+    rows_q = exchange(waiting[0])
     scratch_q = (
         pltpu.VMEM((2, 2 * DH, 2 * FH), BF),
         pltpu.VMEM((2 * FH, 2 * DH), BF),

time: 154 us -> 163 us (1.058)
  waiting for transfers between devices: 31.3 us -> 37.5 us
  starting transfers between devices: 34.3 us -> 36.5 us
    ppermute x1, waiting for transfers between devices: 0.01 us -> 6.17 us  [program(): passed = lax.ppermute(first, 'block', [(b, b + 1) for b in range(size - 1)])]
    all_to_all x3, starting transfers between devices: 21.8 us -> 24.6 us  [exchange(): lax.all_to_all(rows.reshape(-1, 2 * DH), 'tok', split_axis=0, concat_axis...]
    unnamed x18 -> x22, local copies, waits for them, and re-layouts: 2.88 us -> 3.62 us
  transfers between devices with their start and end apart: 8 -> 8, of which waited for: 3 -> 4; matrix products, arithmetic and copies ran while one was open for 1% -> 1% of each run, Pallas kernels for 24% -> 16%
where the time goes in v5:
time: 163 us; the launch traced here: 162 us
  Pallas kernels  50.8 us (31%)
  waiting for transfers between devices  37.5 us (23%)
  starting transfers between devices  36.5 us (22%)
  blocking collectives  31.4 us (19%)
  local copies, waits for them, and re-layouts  4.63 us (3%)
    pallas_call x11, Pallas kernels, call(): pl.pallas_call(kernel, out_shape=outs, in_specs=[pl.BlockSpec(memory_spac...  50.8 us
    all_to_all x1, blocking collectives, exchange(): lax.all_to_all(rows.reshape(-1, 2 * DH), 'tok', split_axis=0, concat_axis...  31.4 us
    all_to_all x3, starting transfers between devices, exchange(): lax.all_to_all(rows.reshape(-1, 2 * DH), 'tok', split_axis=0, concat_axis...  24.6 us
    all_to_all x3, waiting for transfers between devices, exchange(): lax.all_to_all(rows.reshape(-1, 2 * DH), 'tok', split_axis=0, concat_axis...  20.6 us
    ppermute x2, waiting for transfers between devices, advance(): below = lax.ppermute(up, 'tok', UPS)  8.35 us
    ppermute x2, starting transfers between devices, advance(): below = lax.ppermute(up, 'tok', UPS)  6.63 us
    ppermute x1, waiting for transfers between devices, program(): passed = lax.ppermute(first, 'block', [(b, b + 1) for b in range(size - 1)])  6.17 us
    ppermute x2, starting transfers between devices, advance(): above = lax.ppermute(down, 'tok', DOWNS)  3.97 us
  transfers between devices with their start and end apart: 8, of which 4 were waited for; matrix products, arithmetic and copies ran while one was open for 1% of the time, Pallas kernels for 16%

profile of v5, /device:TPU:7, one launch (start us, length us, event | category | flops | bytes accessed | tf_op | source)
XLA Modules:
  0.0 161.9 jit_solution(7512219293855288538)
XLA Ops:
  2.1 3.7 %shard_map.147 = bf16[32,224,128]{2,1,0:T(8,128)(2,1)} custom-call(s32[2,20]{1,0:T(2,128)S(1)} %bitcast.36, s32[20]{0:T(128)S(1)} %copy-done.7, bf16[2,256,1280]{2,1,0:T(8,128)(2,1)} %bitcast.28, bf16[2,256,1280]{2,1,0:T(8,128)(2,1)} %bitcast.30, bf16[20,2,256]{2,1,0:T(2,128)(2,1)} %bitcast.34, bf16[20,16,64]{2,1,0:T(8,128)(2,1)} %bitcast.38, ...), custom_call_target="tpu_custom_call" | custom-call | tf_op jit(solution)/shard_map/pallas_call | solution.py:353
  5.8 9.0 %all-to-all-start = ((bf16[32,224,128]{2,1,0:T(8,128)(2,1)}), bf16[32,224,128]{2,1,0:T(8,128)(2,1)}, u32[]{:S(2)}, u32[]{:S(2)}) async-start(bf16[32,224,128]{2,1,0:T(8,128)(2,1)} %shard_map.147), calls=%async_computation | async-start | bytes 3670016 | tf_op jit(solution)/shard_map/all_to_all | solution.py:368
  14.8 1.4 copy-done.3
  16.3 1.0 shard_map.149
  17.3 2.7 %shard_map.148 = bf16[32,264,128]{2,1,0:T(8,128)(2,1)} custom-call(s32[2,20]{1,0:T(2,128)S(1)} %bitcast.37, s32[20]{0:T(128)S(1)} %copy-done.8, bf16[2,256,1280]{2,1,0:T(8,128)(2,1)S(1)} %bitcast.29, bf16[2,256,1280]{2,1,0:T(8,128)(2,1)S(1)} %bitcast.31, bf16[20,2,256]{2,1,0:T(2,128)(2,1)S(1)} %bitcast.35, bf16[2,256,1280]{2,1,0:T(8,128)(2,1)S(1)} %bitcast.33), custom_call_target="tpu_custom_call" | custom-call | tf_op jit(solution)/shard_map/pallas_call | solution.py:353
  20.0 20.6 %all-to-all-done.rows_hbm = bf16[32,224,128]{2,1,0:T(8,128)(2,1)} async-done(((bf16[32,224,128]{2,1,0:T(8,128)(2,1)}), bf16[32,224,128]{2,1,0:T(8,128)(2,1)}, u32[]{:S(2)}, u32[]{:S(2)}) %all-to-all-start) | async-done | bytes 1835040 | tf_op jit(solution)/shard_map/all_to_all | solution.py:368
  40.6 5.9 %all-to-all-start.1 = ((bf16[32,264,128]{2,1,0:T(8,128)(2,1)}), bf16[32,264,128]{2,1,0:T(8,128)(2,1)}, u32[]{:S(2)}, u32[]{:S(2)}) async-start(bf16[32,264,128]{2,1,0:T(8,128)(2,1)} %shard_map.148), calls=%async_computation.1 | async-start | bytes 4325376 | tf_op jit(solution)/shard_map/all_to_all | solution.py:368
  46.6 1.8 %shard_map.150 = (bf16[2,64,1536]{2,1,0:T(8,128)(2,1)S(1)}, s32[2,512]{1,0:T(2,128)S(1)}) custom-call(s32[2]{0:T(128)S(1)} %pad_add_fusion.role_ref, bf16[32,224,128]{2,1,0:T(8,128)(2,1)} %all-to-all-done.rows_hbm), custom_call_target="tpu_custom_call" | custom-call | tf_op jit(solution)/shard_map/pallas_call | solution.py:353
  48.4 10.6 %shard_map.151 = (bf16[2,64,1536]{2,1,0:T(8,128)(2,1)S(1)}, bf16[64,1536]{1,0:T(8,128)(2,1)S(1)}, bf16[64,1536]{1,0:T(8,128)(2,1)S(1)}) custom-call(s32[2]{0:T(128)S(1)} %pad_add_fusion.role_ref, s32[2,512]{1,0:T(2,128)S(1)} %get-tuple-element.34.counts_ref, s32[20]{0:T(128)S(1)} %copy-done.8, bf16[32,224,128]{2,1,0:T(8,128)(2,1)} %all-to-all-done.rows_hbm, ...), custom_call_target="tpu_custom_call" | custom-call | tf_op jit(solution)/shard_map/pallas_call | solution.py:353
  59.1 3.1 %collective-permute-start = (bf16[64,1536]{1,0:T(8,128)(2,1)S(1)}, bf16[64,1536]{1,0:T(8,128)(2,1)S(1)}, u32[]{:S(2)}, u32[]{:S(2)}) collective-permute-start(bf16[64,1536]{1,0:T(8,128)(2,1)S(1)} %get-tuple-element.38), channel_id=1, source_target_pairs={{0,1},{1,2},{3,4},{4,5},{6,7},{7,8},{9,10},{10,11},{12,13},{13,14}... | collective-permute-start | bytes 589832 | tf_op jit(solution)/shard_map/ppermute | solution.py:410
  62.2 1.9 %collective-permute-start.1 = (bf16[64,1536]{1,0:T(8,128)(2,1)S(1)}, bf16[64,1536]{1,0:T(8,128)(2,1)S(1)}, u32[]{:S(2)}, u32[]{:S(2)}) collective-permute-start(bf16[64,1536]{1,0:T(8,128)(2,1)S(1)} %get-tuple-element.39), channel_id=1, source_target_pairs={{1,0},{2,1},{4,3},{5,4},{7,6},{8,7},{10,9},{11,10},{13,12},{14,13}... | collective-permute-start | bytes 589832 | tf_op jit(solution)/shard_map/ppermute | solution.py:411
  64.1 8.3 %collective-permute-done.below_ref = bf16[64,1536]{1,0:T(8,128)(2,1)S(1)} collective-permute-done((bf16[64,1536]{1,0:T(8,128)(2,1)S(1)}, bf16[64,1536]{1,0:T(8,128)(2,1)S(1)}, u32[]{:S(2)}, u32[]{:S(2)}) %collective-permute-start) | collective-permute-done | bytes 196640 | tf_op jit(solution)/shard_map/ppermute | solution.py:410
  72.4 2.4 %collective-permute-done.1.above_ref = bf16[64,1536]{1,0:T(8,128)(2,1)S(1)} collective-permute-done((bf16[64,1536]{1,0:T(8,128)(2,1)S(1)}, bf16[64,1536]{1,0:T(8,128)(2,1)S(1)}, u32[]{:S(2)}, u32[]{:S(2)}) %collective-permute-start.1) | collective-permute-done | bytes 196640 | tf_op jit(solution)/shard_map/ppermute | solution.py:411
  75.8 1.3 collective-permute-start.2
  77.1 1.0 constant_dynamic-slice_fusion
  78.1 6.2 %collective-permute-done.2 = bf16[2,64,1536]{2,1,0:T(8,128)(2,1)S(1)} collective-permute-done((bf16[2,64,1536]{2,1,0:T(8,128)(2,1)S(1)}, bf16[2,64,1536]{2,1,0:T(8,128)(2,1)S(1)}, u32[]{:S(2)}, u32[]{:S(2)}) %collective-permute-start.2) | collective-permute-done | bytes 393248 | tf_op jit(solution)/shard_map/ppermute | solution.py:424
  84.4 12.0 %shard_map.153 = (bf16[2,64,1536]{2,1,0:T(8,128)(2,1)S(1)}, bf16[64,1536]{1,0:T(8,128)(2,1)}, bf16[64,1536]{1,0:T(8,128)(2,1)}) custom-call(s32[2]{0:T(128)S(1)} %pad_add_fusion.role_ref, s32[2,512]{1,0:T(2,128)S(1)} %get-tuple-element.34.counts_ref, s32[20]{0:T(128)S(1)} %copy-done.8, bf16[32,264,128]{2,1,0:T(8,128)(2,1)} %all-to-all-done.1.rows_hbm.rows_ref, ...), custom_call_target="tpu_custom_call" | custom-call | tf_op jit(solution)/shard_map/pallas_call | solution.py:353
  97.2 9.7 %all-to-all-start.2 = ((bf16[32,88,128]{2,1,0:T(8,128)(2,1)}), bf16[32,88,128]{2,1,0:T(8,128)(2,1)S(1)}, u32[]{:S(2)}, u32[]{:S(2)}) async-start(bf16[32,88,128]{2,1,0:T(8,128)(2,1)} %shard_map.149), calls=%async_computation.2 | async-start | bytes 1441792 | tf_op jit(solution)/shard_map/all_to_all | solution.py:368
  106.9 3.5 %collective-permute-start.3 = (bf16[64,1536]{1,0:T(8,128)(2,1)}, bf16[64,1536]{1,0:T(8,128)(2,1)S(1)}, u32[]{:S(2)}, u32[]{:S(2)}) collective-permute-start(bf16[64,1536]{1,0:T(8,128)(2,1)} %get-tuple-element.44), channel_id=1, source_target_pairs={{0,1},{1,2},{3,4},{4,5},{6,7},{7,8},{9,10},{10,11},{12,13},{13,14}... | collective-permute-start | bytes 589832 | tf_op jit(solution)/shard_map/ppermute | solution.py:410
  110.5 2.1 %collective-permute-start.4 = (bf16[64,1536]{1,0:T(8,128)(2,1)}, bf16[64,1536]{1,0:T(8,128)(2,1)S(1)}, u32[]{:S(2)}, u32[]{:S(2)}) collective-permute-start(bf16[64,1536]{1,0:T(8,128)(2,1)} %get-tuple-element.45), channel_id=1, source_target_pairs={{1,0},{2,1},{4,3},{5,4},{7,6},{8,7},{10,9},{11,10},{13,12},{14,13}... | collective-permute-start | bytes 589832 | tf_op jit(solution)/shard_map/ppermute | solution.py:411
  112.5 8.1 %shard_map.155.refs_0_ = bf16[32,88,128]{2,1,0:T(8,128)(2,1)S(1)} custom-call(s32[2]{0:T(128)S(1)} %pad_add_fusion.role_ref, bf16[32,264,128]{2,1,0:T(8,128)(2,1)} %all-to-all-done.1.rows_hbm.rows_ref, bf16[2,64,1536]{2,1,0:T(8,128)(2,1)S(1)} %shard_map.152.weights_ref), custom_call_target="tpu_custom_call" | custom-call | tf_op jit(solution)/shard_map/pallas_call | solution.py:353
  121.7 7.4 %shard_map.156 = bf16[32,208,128]{2,1,0:T(8,128)(2,1)S(1)} custom-call(s32[2]{0:T(128)S(1)} %pad_add_fusion.role_ref, bf16[32,88,128]{2,1,0:T(8,128)(2,1)S(1)} %all-to-all-done.2.rows_ref, bf16[2,64,1536]{2,1,0:T(8,128)(2,1)S(1)} %shard_map.154.weights_ref, bf16[32,88,128]{2,1,0:T(8,128)(2,1)S(1)} %shard_map.155.refs_0_), custom_call_target="tpu_custom_call" | custom-call | tf_op jit(solution)/shard_map/pallas_call | solution.py:353
  129.0 31.4 %all_to_all.24.rows_ref = bf16[32,208,128]{2,1,0:T(8,128)(2,1)S(1)} all-to-all(bf16[32,208,128]{2,1,0:T(8,128)(2,1)S(1)} %shard_map.156), channel_id=1, replica_groups=mesh['block'=4,'tok'=32] {'tok'}, dimensions={0} | all-to-all | bytes 3407872 | tf_op jit(solution)/shard_map/all_to_all | solution.py:368
  160.4 1.5 shard_map.157
  (30 shorter events, 4.3 us)
Async XLA Ops:
  0.6 76.5 %copy-start = (bf16[20,64,512]{2,1,0:T(8,128)(2,1)S(1)}, bf16[20,64,512]{2,1,0:T(8,128)(2,1)}, u32[]{:S(2)}) copy-start(bf16[20,64,512]{2,1,0:T(8,128)(2,1)} %param.21) | copy-start | bytes 3932164
  0.6 0.8 copy-start.7
  1.4 0.7 copy-start.9
  5.8 11.5 %copy-start.2 = (bf16[1,2,256,1280]{3,2,1,0:T(8,128)(2,1)S(1)}, bf16[1,2,256,1280]{3,2,1,0:T(8,128)(2,1)}, u32[]{:S(2)}) copy-start(bf16[1,2,256,1280]{3,2,1,0:T(8,128)(2,1)} %param.13) | copy-start | bytes 3932164
  5.8 34.7 %all-to-all-start = ((bf16[32,224,128]{2,1,0:T(8,128)(2,1)}), bf16[32,224,128]{2,1,0:T(8,128)(2,1)}, u32[]{:S(2)}, u32[]{:S(2)}) async-start(bf16[32,224,128]{2,1,0:T(8,128)(2,1)} %shard_map.147), calls=%async_computation | async-start | bytes 3670016 | tf_op jit(solution)/shard_map/all_to_all | solution.py:368
  14.8 2.5 %copy-start.1 = (bf16[1,2,256,1280]{3,2,1,0:T(8,128)(2,1)S(1)}, bf16[1,2,256,1280]{3,2,1,0:T(8,128)(2,1)}, u32[]{:S(2)}) copy-start(bf16[1,2,256,1280]{3,2,1,0:T(8,128)(2,1)} %param.12) | copy-start | bytes 3932164
  14.8 1.4 copy-start.3
  16.3 1.0 copy-start.6
  16.3 1.0 copy-start.8
  16.3 1.1 copy-start.10
  40.6 43.8 %all-to-all-start.1 = ((bf16[32,264,128]{2,1,0:T(8,128)(2,1)}), bf16[32,264,128]{2,1,0:T(8,128)(2,1)}, u32[]{:S(2)}, u32[]{:S(2)}) async-start(bf16[32,264,128]{2,1,0:T(8,128)(2,1)} %shard_map.148), calls=%async_computation.1 | async-start | bytes 4325376 | tf_op jit(solution)/shard_map/all_to_all | solution.py:368
  59.1 13.4 %collective-permute-start = (bf16[64,1536]{1,0:T(8,128)(2,1)S(1)}, bf16[64,1536]{1,0:T(8,128)(2,1)S(1)}, u32[]{:S(2)}, u32[]{:S(2)}) collective-permute-start(bf16[64,1536]{1,0:T(8,128)(2,1)S(1)} %get-tuple-element.38), channel_id=1, source_target_pairs={{0,1},{1,2},{3,4},{4,5},{6,7},{7,8},{9,10},{10,11},{12,13},{13,14}... | collective-permute-start | bytes 589832 | tf_op jit(solution)/shard_map/ppermute | solution.py:410
  62.2 12.6 %collective-permute-start.1 = (bf16[64,1536]{1,0:T(8,128)(2,1)S(1)}, bf16[64,1536]{1,0:T(8,128)(2,1)S(1)}, u32[]{:S(2)}, u32[]{:S(2)}) collective-permute-start(bf16[64,1536]{1,0:T(8,128)(2,1)S(1)} %get-tuple-element.39), channel_id=1, source_target_pairs={{1,0},{2,1},{4,3},{5,4},{7,6},{8,7},{10,9},{11,10},{13,12},{14,13}... | collective-permute-start | bytes 589832 | tf_op jit(solution)/shard_map/ppermute | solution.py:411
  75.8 8.5 %collective-permute-start.2 = (bf16[2,64,1536]{2,1,0:T(8,128)(2,1)S(1)}, bf16[2,64,1536]{2,1,0:T(8,128)(2,1)S(1)}, u32[]{:S(2)}, u32[]{:S(2)}) collective-permute-start(bf16[2,64,1536]{2,1,0:T(8,128)(2,1)S(1)} %shard_map.152.weights_ref), channel_id=1, source_target_pairs={{0,32},{32,64},{64,96},{1,33},{33,65},{65,97},{2,34},{34,66},{66,9... | collective-permute-start | bytes 1179656 | tf_op jit(solution)/shard_map/ppermute | solution.py:424
  96.4 0.7 copy-start.4
  97.2 24.5 %all-to-all-start.2 = ((bf16[32,88,128]{2,1,0:T(8,128)(2,1)}), bf16[32,88,128]{2,1,0:T(8,128)(2,1)S(1)}, u32[]{:S(2)}, u32[]{:S(2)}) async-start(bf16[32,88,128]{2,1,0:T(8,128)(2,1)} %shard_map.149), calls=%async_computation.2 | async-start | bytes 1441792 | tf_op jit(solution)/shard_map/all_to_all | solution.py:368
  106.9 13.8 %collective-permute-start.3 = (bf16[64,1536]{1,0:T(8,128)(2,1)}, bf16[64,1536]{1,0:T(8,128)(2,1)S(1)}, u32[]{:S(2)}, u32[]{:S(2)}) collective-permute-start(bf16[64,1536]{1,0:T(8,128)(2,1)} %get-tuple-element.44), channel_id=1, source_target_pairs={{0,1},{1,2},{3,4},{4,5},{6,7},{7,8},{9,10},{10,11},{12,13},{13,14}... | collective-permute-start | bytes 589832 | tf_op jit(solution)/shard_map/ppermute | solution.py:410
  110.4 10.2 %copy-start.5 = (bf16[2,64,1536]{2,1,0:T(8,128)(2,1)S(1)}, bf16[2,64,1536]{2,1,0:T(8,128)(2,1)}, u32[]{:S(2)}) copy-start(bf16[2,64,1536]{2,1,0:T(8,128)(2,1)} %copy-done.4) | copy-start | bytes 1179652
  110.5 10.2 %collective-permute-start.4 = (bf16[64,1536]{1,0:T(8,128)(2,1)}, bf16[64,1536]{1,0:T(8,128)(2,1)S(1)}, u32[]{:S(2)}, u32[]{:S(2)}) collective-permute-start(bf16[64,1536]{1,0:T(8,128)(2,1)} %get-tuple-element.45), channel_id=1, source_target_pairs={{1,0},{2,1},{4,3},{5,4},{7,6},{8,7},{10,9},{11,10},{13,12},{14,13}... | collective-permute-start | bytes 589832 | tf_op jit(solution)/shard_map/ppermute | solution.py:411
